TPU v7x, 256 devices: a whole 4x4x8 slice. The times are simulated.
256 devices in a mesh: region: 4 (over z_hi), tile: 64 (over z_lo, y, x, core).
Axes of the slice: x: 4, y: 4, z: 8 (z_hi: 4, z_lo: 2; z = z_hi * 2 + z_lo), core: 2. Of those that a mesh axis runs over, the one named last changes fastest.
Arguments:
- global_field: bfloat16 [70, 512, 1280], P(None, 'tile', 'region'), may hold values from -6 to 6
- regional_state: bfloat16 [256, 99, 64, 128], P(('region', 'tile')), may hold values from -6 to 6
- windows: int32 [8, 4], replicated, may hold values from 0 to 1152, as said below
- longitude_weights: bfloat16 [8, 512, 128], replicated, may hold values from -0.75 to 0.75
- latitude_weights: bfloat16 [8, 512, 64], P('region'), may hold values from -1 to 1
- first_kernel: bfloat16 [3, 3, 96, 169], replicated, may hold values from -0.15625 to 0.15625
- first_bias: float32 [96], replicated, may hold values from -3 to 3
- second_kernel: bfloat16 [3, 3, 96, 96], replicated, may hold values from -0.21875 to 0.21875
- later_conv_bias: float32 [96], replicated, may hold values from -3 to 3
- shortcut_weight: bfloat16 [96, 169], replicated, may hold values from -0.5 to 0.5
Outputs:
- block_output: bfloat16 [256, 96, 64, 128], P(('region', 'tile'))
Inputs may be any that keep to these rules, and one draw needn't show every extreme that they name: `windows`: columns per domain: latitude start 0 to 448, latitude rows used 64 // 2 to 64, longitude start 0 to 1152, longitude columns used 128 // 2 to 128; some domain uses all 64 rows and some all 128 columns.
All inputs are finite; a program needn't handle non-finite values.
Results may differ from a plain program's by a relative error of at most 0.0053.
Values may be sent and summed in bfloat16 or wider, within the bound.
No kernel may reach another device: no remote copies, remote signals or barrier semaphores. Data moves between devices by JAX's collectives and lax.ppermute only.
A program may use at most 128 MiB of HBM per device.

v0:
```python
import jax
import jax.numpy as jnp
import numpy as np
from jax import lax
from jax.experimental import pallas as pl
from jax.experimental.pallas import tpu as pltpu
from jax.sharding import PartitionSpec as P


TCOLS = 4
ROWS = 8
EVERY = ("region", "tile")
SP = 112
CP = 80
WP = 72
YP = 72
F32, BF16 = jnp.float32, jnp.bfloat16


def mm(a, b):
    return jnp.dot(a, b, preferred_element_type=F32)


def mm_t(a, b):
    return lax.dot_general(a, b, (((1,), (1,)), ((), ())), preferred_element_type=F32)


def iota(shape, dim):
    return lax.broadcasted_iota(jnp.int32, shape, dim)


def chosen(cond):
    return jnp.where(cond, 1.0, 0.0).astype(BF16)


def column(row):
    n = row.shape[1]
    hit = iota((n, n), 0) == iota((n, n), 1)
    return jnp.sum(jnp.where(hit, row, 0.0), axis=1, keepdims=True)


def rows_at(start, size, unit):
    return pl.ds(pl.multiple_of(start, unit), size)


def along(parts, och):
    return (
        parts[:och]
        + pltpu.roll(parts[och : 2 * och], 127, 1)
        + pltpu.roll(parts[2 * och : 3 * och], 126, 1)
    )


def across(parts, edges, at, och):
    lane = iota((och, 128), 1)
    west = jnp.where(lane == 0, pltpu.roll(edges[0], 128 - at, 1), pltpu.roll(parts[:och], 1, 1))
    east = jnp.where(
        lane == 127, pltpu.roll(edges[1], 127 - at, 1), pltpu.roll(parts[2 * och : 3 * och], 127, 1)
    )
    return parts[och : 2 * och] + west + east


def stacked(k3, q, och):
    return jnp.concatenate([k3[p, q * och : (q + 1) * och, :] for p in range(3)], axis=0)


def turn_body(state, xs, strips, flat, packs):
    chans, height = state.shape[0], state.shape[1]

    def widen(c, _):
        flat[rows_at(YP * c, height, 8), :] = state[c].astype(F32)
        return 0

    lax.fori_loop(0, chans, widen, 0, unroll=3)
    flat[pl.ds(YP * chans, YP * (SP - chans)), :] = jnp.zeros((YP * (SP - chans), 128), F32)

    def row(y, _):
        xs[rows_at(SP * y, SP, 16), :] = flat[pl.ds(y, SP, stride=YP), :].astype(BF16)
        return 0

    lax.fori_loop(0, height, row, 0, unroll=4)
    lane = iota((height, 128), 1)
    for b in range(4):
        packed = jnp.zeros((height, 128), F32)
        for c in range(min(32, chans - 32 * b)):
            one = pltpu.roll(flat[pl.ds(YP * (32 * b + c), height), :], (2 + 4 * c) % 128, 1)
            packed = jnp.where(lane // 4 == c, one, packed)
        packed = jnp.concatenate([packed, jnp.zeros((128 - height, 128), F32)], axis=0)
        packs[pl.ds(128 * b, 128), :] = packed.T
    for col in range(4):
        for b in range(4):
            n = min(32, SP - 32 * b)
            strips[pl.ds(SP * col + 32 * b, n), :] = packs[
                pl.ds(128 * b + col, n, stride=4), :
            ].astype(BF16)


def corner_body(scal, strips, above, below, ext):
    lane = iota((SP, 128), 1)
    top, bottom = scal[0] > 0, scal[1] > 0
    for j, x in enumerate((126, 127, 0, 1)):
        e = pltpu.roll(strips[pl.ds(SP * j, SP), :].astype(F32), 2, 1)
        for m in range(2):
            up = pltpu.roll(above[pl.ds(SP * m, SP), :].astype(F32), (m - x) % 128, 1)
            down = pltpu.roll(below[pl.ds(SP * m, SP), :].astype(F32), (66 + m - x) % 128, 1)
            e = jnp.where((lane == m) & top, up, e)
            e = jnp.where((lane == 66 + m) & bottom, down, e)
        ext[pl.ds(SP * j, SP), :] = e.astype(BF16)


def early_body(
    scal, xs_own, above, below, ext, west, east, k1, sw, k2, lon, lat, rho, b1, b2,
    acc, skip, side, w1c, v1c, e1c, w2, lonb, latb,
    xs, w1s, sem,
):
    och = sw.shape[0]
    cin = sw.shape[1]
    sch = cin - 70
    fetch = pltpu.make_async_copy(xs_own, xs.at[pl.ds(2 * SP, 64 * SP)], sem)
    fetch.start()
    top, bottom, left, right = scal[0] > 0, scal[1] > 0, scal[2] > 0, scal[3] > 0
    xs[pl.ds(0, 2 * SP), :] = jnp.where(top, above[...], 0)
    xs[pl.ds(66 * SP, 2 * SP), :] = jnp.where(bottom, below[...], 0)
    bias1, bias2 = column(b1[...]), column(b2[...])

    row_s, col_s = iota((cin, 3 * SP), 0), iota((cin, 3 * SP), 1)
    row_c, col_c = iota((cin, 3 * CP), 0), iota((cin, 3 * CP), 1)
    put_s = [chosen((col_s == SP * p + row_s) & (row_s < sch)) for p in range(3)]
    put_c = [chosen((col_c == CP * p + row_c - sch) & (row_c >= sch)) for p in range(3)]
    w1s[pl.ds(0, 3 * och), :] = sum(mm(k1[p], put_s[p]) for p in range(3)).astype(BF16)
    w1s[pl.ds(3 * och, och), :] = mm(sw[...], put_s[1]).astype(BF16)
    w1c[pl.ds(0, 3 * och), :] = sum(mm(k1[p], put_c[p]) for p in range(3)).astype(BF16)
    w1c[pl.ds(3 * och, och), :] = mm(sw[...], put_c[1]).astype(BF16)
    turned = [stacked(k1, q, och) for q in range(3)]
    v1s = sum(mm(turned[q], put_s[q]) for q in range(3)).astype(BF16)
    v1c[...] = sum(mm(turned[q], put_c[q]) for q in range(3)).astype(BF16)
    row_e, col_e = iota((cin, CP), 0), iota((cin, CP), 1)
    put_e = chosen((col_e == row_e - sch) & (row_e >= sch))
    e1c[0] = mm(turned[0], put_e).astype(BF16)
    e1c[1] = mm(turned[2], put_e).astype(BF16)
    row_2, col_2 = iota((och, 3 * och), 0), iota((och, 3 * och), 1)
    w2[...] = sum(mm(k2[p], chosen(col_2 == och * p + row_2)) for p in range(3)).astype(BF16)

    masked = jnp.where(iota((512, 128), 1) < scal[8], lon[0], 0)
    r, c = iota((256, 512), 0), iota((256, 512), 1)
    six = (r - 128) % 8
    off = jnp.where(r < 128, r, jnp.where(six < 3, six - 2, six + 124))
    pick = chosen((c == off + 128 * scal[5]) & ((r < 128) | (six < 6)))
    lonb[...] = mm(pick, masked).astype(BF16)
    r, c = iota((128, 512), 0), iota((128, 512), 1)
    pick = chosen((c == r - 2 + 64 * scal[4]) & (r < 68))
    taken = mm(pick, lat[0]).astype(BF16)
    want = (rho[...] - scal[6]) & 63
    order = chosen((iota((64, 64), 0) == want) & (want < scal[7]))
    latb[...] = mm(taken, order).astype(BF16)

    west_in = jnp.where(left, west[...], 0)
    east_in = jnp.where(right, east[...], 0)
    ps = jnp.concatenate(
        [
            jnp.concatenate([west_in, ext[pl.ds(2 * SP, SP), :]], axis=0),
            jnp.concatenate([ext[pl.ds(SP, SP), :], east_in], axis=0),
        ],
        axis=1,
    )
    got = mm(v1s, ps)
    for s in range(2):
        side[:, 128 * s : 128 * s + 128] = along(got[:, 128 * s : 128 * s + 128], och) + bias1
    edges = [
        along(mm(turned[0][:, :SP], west_in[SP:]), och),
        along(mm(turned[2][:, :SP], east_in[:SP]), och),
    ]
    fetch.wait()

    def conv(i, _):
        rows = [xs[rows_at(SP * (2 * i + m), 3 * SP, 16), :] for m in range(2)]
        got = mm(w1s[...], jnp.concatenate(rows, axis=1))
        for m in range(2):
            parts = got[:, 128 * m : 128 * m + 128]
            at = rows_at(och * (2 * i + m), och, 16)
            acc[at, :] = across(parts, edges, 2 * i + m, och) + bias1
            skip[at, :] = parts[3 * och :] + bias2
        return 0

    lax.fori_loop(0, 33, conv, 0)


def late_body(
    scal, wa, wb, lonb, latb, w1c, v1c, e1c, w2, k2, side, acc_hbm, skip_hbm,
    out, bands, sideb, cf, ch, cs, pc, hid, acc, skip, edge1, edge2, of, sems,
):
    och = side.shape[0]
    half = wa.shape[0]
    step = 288
    fetch = [
        pltpu.make_async_copy(acc_hbm, acc, sems.at[0]),
        pltpu.make_async_copy(skip_hbm, skip, sems.at[1]),
    ]
    for copy in fetch:
        copy.start()

    def spread(k, _):
        at = pl.multiple_of(k * step, 16)
        for base, part in ((0, wa), (half, wb)):
            got = mm_t(part[pl.ds(at, step), :], lonb[...])
            to = rows_at(base + at, step, 16)
            bands[to, :] = got[:, :128]
            sideb[to, :] = got[:, 128:]
        return 0

    lax.fori_loop(0, half // step, spread, 0)

    def rows(k, _):
        pair = [bands[pl.ds(2 * k + m, 64, stride=WP), :].astype(BF16) for m in range(2)]
        got = mm(latb[pl.ds(0, YP), :], jnp.concatenate(pair, axis=1))
        cf[rows_at(2 * k * YP, YP, 8), :] = got[:, :128]
        cf[rows_at((2 * k + 1) * YP, YP, 8), :] = got[:, 128:]
        return 0

    lax.fori_loop(0, WP // 2, rows, 0, unroll=6)

    lane = iota((64, 128), 1)
    for b in range(CP // 16):
        packed = jnp.zeros((64, 128), F32)
        for c in range(min(16, WP - 16 * b)):
            one = sideb[pl.ds(16 * b + c, 64, stride=WP), :]
            packed = jnp.where(lane // 8 == c, one, packed)
        ch[pl.ds(128 * b, 128), :] = mm_t(packed.T.astype(BF16), latb[...])
    for x in range(6):
        s, k = x // 3, x % 3
        for b in range(CP // 16):
            pc[pl.ds(CP * k + 16 * b, 16), pl.ds(128 * s, 128)] = ch[
                pl.ds(128 * b + x, 16, stride=8), :
            ].astype(BF16)

    def turn(y, _):
        one = cf[pl.ds(y, WP, stride=YP), :]
        one = jnp.concatenate([one, jnp.zeros((CP - WP, 128), F32)], axis=0)
        cs[rows_at(CP * y, CP, 16), :] = one.astype(BF16)
        return 0

    lax.fori_loop(0, 68, turn, 0, unroll=4)

    lane = iota((och, 128), 1)
    got = mm(v1c[...], pc[...])
    for s in range(2):
        lanes = pl.ds(128 * s, 128)
        v = along(got[:, 128 * s : 128 * s + 128], och) + side[:, lanes]
        v = v / (1.0 + jnp.exp(-v))
        keep = (
            ((lane > 0) | (scal[0] > 0))
            & ((lane < 65) | (scal[1] > 0))
            & (lane < 66)
            & (scal[2 + s] > 0)
        )
        v = jnp.where(keep, v, 0.0).astype(BF16)
        edge2[s] = along(mm(stacked(k2, 2 * s, och), v), och)
        edge1[s] = along(mm(e1c[s], pc[pl.ds(CP, CP), lanes]), och)
    for copy in fetch:
        copy.wait()

    def conv1(i, _):
        r = 2 * i
        cond = [cs[rows_at(CP * (r + m), 3 * CP, 16), :] for m in range(2)]
        got = mm(w1c[...], jnp.concatenate(cond, axis=1))
        for m in range(2):
            parts = got[:, 128 * m : 128 * m + 128]
            at = rows_at(och * (r + m), och, 16)
            v = across(parts, edge1, r + m, och) + acc[at, :]
            v = v / (1.0 + jnp.exp(-v))
            live = jnp.where(r + m == 0, scal[0], jnp.where(r + m == 65, scal[1], 1))
            hid[at, :] = (v * live.astype(F32)).astype(BF16)
            skip[at, :] = skip[at, :] + parts[3 * och :]
        return 0

    lax.fori_loop(0, 33, conv1, 0)

    def conv2(j, _):
        y = 2 * j
        above = [hid[rows_at(och * (y + m), 3 * och, 16), :] for m in range(2)]
        got = mm(w2[...], jnp.concatenate(above, axis=1))
        for m in range(2):
            v = across(got[:, 128 * m : 128 * m + 128], edge2, y + m, och)
            of[pl.ds(y + m, och, stride=YP), :] = v + skip[rows_at(och * (y + m + 1), och, 16), :]
        return 0

    lax.fori_loop(0, 32, conv2, 0)

    def leave(o, _):
        out[o] = of[rows_at(YP * o, 64, 8), :].astype(BF16)
        return 0

    lax.fori_loop(0, och, leave, 0, unroll=4)


def pick_body(scal, rows, out):
    lon = rows.shape[2]
    for d in range(8):
        hit = chosen(iota((lon, 128), 0) == iota((lon, 128), 1) + scal[8 + d])
        got = mm(rows[scal[d]], hit)
        out[d] = jnp.concatenate([got, jnp.zeros((WP - got.shape[0], 128), F32)], axis=0).astype(BF16)


def call(body, outs, scratch, args, specs=None, scalars=0, flops=10**7, vmem=48):
    def whole(shape):
        zeros = (0,) * len(shape)
        return pl.BlockSpec(shape, lambda i, *_: zeros, pipeline_mode=pl.Buffered(1))

    specs = specs or {}
    arrays = args[scalars:]
    return pl.pallas_call(
        body,
        grid_spec=pltpu.PrefetchScalarGridSpec(
            num_scalar_prefetch=scalars,
            grid=(1,),
            in_specs=[specs.get(n) or whole(a.shape) for n, a in enumerate(arrays)],
            out_specs=[whole(o.shape) for o in outs],
            scratch_shapes=scratch,
        ),
        out_shape=outs,
        compiler_params=pltpu.CompilerParams(vmem_limit_bytes=vmem * 2**20),
        cost_estimate=pl.CostEstimate(flops=flops, bytes_accessed=2**20, transcendentals=0),
    )(*args)


def out(shape, dtype=BF16):
    return jax.ShapeDtypeStruct(shape, dtype)


def turned_state(state):
    return call(
        turn_body, [out((64 * SP, 128)), out((4 * SP, 128))],
        [pltpu.VMEM((YP * SP, 128), F32), pltpu.VMEM((512, 128), F32)],
        [state], flops=10**9,
    )


def with_corners(scal, strips, above, below):
    return call(
        corner_body, [out((4 * SP, 128))], [], [scal, strips, above, below],
        scalars=1,
    )[0]


def early(scal, xs, above, below, ext, west, east, k1, sw, k2, lon, lat, rho, b1, b2):
    och, cin = sw.shape
    return call(
        early_body,
        [
            out((66 * och, 128), F32), out((66 * och, 128), F32), out((och, 256), F32),
            out((4 * och, 3 * CP)), out((3 * och, 3 * CP)), out((2, 3 * och, CP)),
            out((3 * och, 3 * och)), out((256, 128)), out((128, 64)),
        ],
        [pltpu.VMEM((68 * SP, 128), BF16), pltpu.VMEM((4 * och, 3 * SP), BF16), pltpu.SemaphoreType.DMA],
        [
            scal, xs, above, below, ext, west, east, k1.reshape(3, 3 * och, cin), sw,
            k2.reshape(3, 3 * och, och), lon, lat, rho, b1[None], b2[None],
        ],
        specs={
            0: pl.BlockSpec(memory_space=pltpu.HBM),
            9: pl.BlockSpec((1, 512, 128), lambda i, s: (s[9], 0, 0)),
            10: pl.BlockSpec((1, 512, 64), lambda i, s: (s[10], 0, 0)),
        },
        scalars=1, flops=6 * 10**9,
    )


def late(scal, wa, wb, k2, parts):
    acc, skip, side, w1c, v1c, e1c, w2, lonb, latb = parts
    och = side.shape[0]
    vm = pltpu.VMEM
    return call(
        late_body, [out((och, 64, 128))],
        [
            vm((64 * WP, 128), F32), vm((64 * WP, 128), F32), vm((WP * YP, 128), F32),
            vm((128 * CP // 16, 128), F32), vm((68 * CP, 128), BF16), vm((3 * CP, 256), BF16),
            vm((66 * och, 128), BF16), vm((66 * och, 128), F32), vm((66 * och, 128), F32),
            vm((2, och, 128), F32), vm((2, och, 128), F32), vm((och * YP, 128), F32),
            pltpu.SemaphoreType.DMA((2,)),
        ],
        [
            scal, wa, wb, lonb, latb, w1c, v1c, e1c, w2, k2.reshape(3, 3 * och, och), side, acc, skip,
        ],
        specs={10: pl.BlockSpec(memory_space=pltpu.HBM), 11: pl.BlockSpec(memory_space=pltpu.HBM)},
        scalars=1, flops=8 * 10**9, vmem=58,
    )[0]


def picked(scal, rows):
    return call(pick_body, [out((8, WP, 128))], [], [scal, rows], scalars=1)[0]


def domain_half(tile, tiles, rotation):
    return ((tile + rotation) % tiles) // (tiles // 2)


def routes(regions, tiles, rotation):
    bands = tiles // ROWS
    half = [[domain_half(ROWS * k + g, tiles, rotation) for k in range(bands)] for g in range(ROWS)]
    by_row, by_domain, rows = [], [], np.zeros((tiles, 2), np.int32)
    for z in range(regions):
        for g in range(ROWS):
            by_row.append([z * tiles + k * ROWS + g for k in range(bands)])
    for g in range(ROWS):
        lower = [k for k in range(bands) if half[g][k] == 0]
        upper = [k for k in range(bands) if half[g][k] == 1]
        for pair in zip(lower, upper):
            by_domain.append([z * tiles + k * ROWS + g for z in range(regions) for k in pair])
            for k in pair:
                rows[k * ROWS + g] = [ROWS * g + pair[0], ROWS * g + pair[1]]
    tile_half = [domain_half(t, tiles, rotation) for t in range(tiles)]
    spread, table = [], np.zeros((2, 2, tiles), np.int32)
    for z in range(regions):
        for h in range(2):
            for core in range(2):
                spread.append([z * tiles + t for t in range(tiles) if tile_half[t] == h and t % 2 == core])
    for h in range(2):
        for core in range(2):
            mine = [t for t in range(tiles) if tile_half[t] == h and t % 2 == core]
            other = [t for t in range(tiles) if tile_half[t] == h and t % 2 != core]
            table[h, core] = np.concatenate([rows[t] for t in mine + other])
    return by_row, by_domain, spread, table


def swap(value, groups):
    return lax.all_to_all(
        value, EVERY, split_axis=0, concat_axis=0, axis_index_groups=groups, tiled=True
    )


def from_neighbour(block, distance):
    size = lax.axis_size("tile")
    return lax.ppermute(block, "tile", [((i - distance) % size, i) for i in range(size)])


def shards(
    global_field,
    regional_state,
    windows,
    longitude_weights,
    latitude_weights,
    first_kernel,
    first_bias,
    second_kernel,
    later_conv_bias,
    shortcut_weight,
):
    tile_count, regions = lax.axis_size("tile"), lax.axis_size("region")
    tile, region = lax.axis_index("tile"), lax.axis_index("region")
    half_count = tile_count // 2
    row_tiles = half_count // TCOLS
    rotation = tile_count // 4 + 2
    position = (tile + rotation) % tile_count
    half, within = position // half_count, position % half_count
    row, col = within // TCOLS, within % TCOLS
    domain = 2 * region + half
    by_row, by_domain, spread, table = routes(regions, tile_count, rotation)

    by_rows = swap(global_field.transpose(1, 0, 2), by_row)

    own = lax.dynamic_index_in_dim(windows, domain, 0, keepdims=False)
    flags = [row > 0, row < row_tiles - 1, col > 0, col < TCOLS - 1]
    scal = jnp.stack([*flags, row, col, own[0], own[1], own[3], domain, half]).astype(jnp.int32)
    rho = lax.dynamic_slice(jnp.asarray(table), (half, tile % 2, 0), (1, 1, 64))[0]

    xs, strips = turned_state(regional_state[0])
    above = from_neighbour(xs[-2 * SP :], TCOLS)
    below = from_neighbour(xs[: 2 * SP], -TCOLS)
    ext = with_corners(scal, strips, above, below)
    residue = ROWS * (tile % ROWS) + tile // ROWS
    source = (windows[:, 0] + (residue - windows[:, 0]) % 64) // 64
    offset = windows[:, 2] - global_field.shape[2] * region
    where, ext = lax.optimization_barrier((jnp.concatenate([source, offset]), ext))
    chosen_parts = picked(where, by_rows)
    west = from_neighbour(ext[: 2 * SP], 1)
    east = from_neighbour(ext[2 * SP :], -1)
    parts = early(
        scal, xs, above, below, ext, west, east, first_kernel, shortcut_weight, second_kernel,
        longitude_weights, latitude_weights, rho, first_bias, later_conv_bias,
    )
    mixed = swap(chosen_parts, by_domain)
    piece = mixed.reshape(regions, 2, *mixed.shape[1:]).astype(jnp.float32).sum(0)
    piece = piece.astype(jnp.bfloat16)
    piece, parts = lax.optimization_barrier((piece, parts))
    sharers = len(spread[0])
    mine = swap(jnp.broadcast_to(piece[None], (sharers, *piece.shape)), spread)
    mine = mine.reshape(-1, piece.shape[-1])
    other = lax.ppermute(mine, EVERY, [(i, i ^ 1) for i in range(regions * tile_count)])
    return late(scal, mine, other, second_kernel, parts)[None]


def solution(mesh):
    placed = (
        P(None, "tile", "region"),
        P(("region", "tile"), None, None, None),
        P(),
        P(),
        P("region", None, None),
        P(),
        P(),
        P(),
        P(),
        P(),
    )
    return jax.shard_map(
        shards,
        mesh=mesh,
        in_specs=placed,
        out_specs=P(("region", "tile"), None, None, None),
        check_vma=False,
    )
```

profile of v0, /device:TPU:32, one launch (start us, length us, event | category | flops | bytes accessed | tf_op | source)
XLA Modules:
  0.0 108.4 jit_solution(17582270320500488198)
XLA Ops:
  0.0 1.4 %copy-done.1 = bf16[1,99,64,128]{3,2,1,0:T(8,128)(2,1)S(1)} copy-done((bf16[1,99,64,128]{3,2,1,0:T(8,128)(2,1)S(1)}, bf16[1,99,64,128]{3,2,1,0:T(8,128)(2,1)}, u32[]{:S(2)}) %copy-start.1) | copy-done | bytes 1622040
  1.4 2.1 %shard_map.109 = (bf16[7168,128]{1,0:T(8,128)(2,1)S(1)}, bf16[448,128]{1,0:T(8,128)(2,1)S(1)}) custom-call(bf16[99,64,128]{2,1,0:T(8,128)(2,1)S(1)} %bitcast.34), custom_call_target="tpu_custom_call" | custom-call | flops 1000000000 | bytes 1048576 | tf_op jit(solution)/shard_map/pallas_call | solution.py:311
  3.6 0.6 fusion.2
  4.2 3.0 %collective-permute-start = (bf16[224,128]{1,0:T(8,128)(2,1)}, bf16[224,128]{1,0:T(8,128)(2,1)S(1)}, u32[]{:S(2)}, u32[]{:S(2)}) collective-permute-start(bf16[224,128]{1,0:T(8,128)(2,1)} %get-tuple-element.52), channel_id=1, source_target_pairs={{60,0},{61,1},{62,2},{63,3},{0,4},{1,5},{2,6},{3,7},{4,8},{5,9},{6... | collective-permute-start | bytes 172040 | tf_op jit(solution)/shard_map/ppermute | solution.py:433
  7.2 3.5 %collective-permute-start.1 = (bf16[224,128]{1,0:T(8,128)(2,1)S(1)}, bf16[224,128]{1,0:T(8,128)(2,1)S(1)}, u32[]{:S(2)}, u32[]{:S(2)}) collective-permute-start(bf16[224,128]{1,0:T(8,128)(2,1)S(1)} %get-tuple-element.51), channel_id=1, source_target_pairs={{4,0},{5,1},{6,2},{7,3},{8,4},{9,5},{10,6},{11,7},{12,8},{13,9},{1... | collective-permute-start | bytes 172040 | tf_op jit(solution)/shard_map/ppermute | solution.py:433
  10.8 0.8 copy.17
  11.6 5.3 %all-to-all-start = ((bf16[8,70,320]{2,1,0:T(8,128)(2,1)}), bf16[8,70,320]{2,1,0:T(8,128)(2,1)S(1)}, u32[]{:S(2)}, u32[]{:S(2)}) async-start(bf16[8,70,320]{2,1,0:T(8,128)(2,1)} %bitcast.32), calls=%async_computation | async-start | bytes 884736 | tf_op jit(solution)/shard_map/all_to_all | solution.py:426
  17.0 0.6 fusion.4
  17.6 0.6 and_select_fusion
  18.1 0.2 copy.13
  18.6 0.9 copy.14.sw
  19.5 2.0 %stack.51.scal = s32[11]{0:T(128)S(1)} concatenate(s32[1]{0:T(128)} %bitcast, s32[1]{0:T(128)} %bitcast.1, s32[1]{0:T(128)} %bitcast.2, s32[1]{0:T(128)} %bitcast.3, s32[1]{0:T(128)} %bitcast.4, s32[1]{0:T(128)} %bitcast.5, s32[1]{0:T(128)} %bitcast.6, s32[1]{0:T(128)} %bitcast.7, s32[1]{0:T(128)} %bitcast.8, s32[1]{0:T(128)} %bitcast.9, s32[1]{0:T(128)} %bitcast.10), dimensions={0} | concatenate | bytes 88 | tf_op jit(solution)/shard_map/stack | solution.py:463
  21.5 0.7 pad_add_fusion.scal
  22.2 0.7 shard_map.110.ext
  23.1 6.0 %collective-permute-start.3 = (bf16[224,128]{1,0:T(8,128)(2,1)S(1)}, bf16[224,128]{1,0:T(8,128)(2,1)S(1)}, u32[]{:S(2)}, u32[]{:S(2)}) collective-permute-start(bf16[224,128]{1,0:T(8,128)(2,1)S(1)} %get-tuple-element.53), channel_id=1, source_target_pairs={{1,0},{2,1},{3,2},{4,3},{5,4},{6,5},{7,6},{8,7},{9,8},{10,9},{11,1... | collective-permute-start | bytes 172040 | tf_op jit(solution)/shard_map/ppermute | solution.py:433
  29.0 0.7 dynamic-slice_bitcast_fusion.rho
  29.7 1.5 %shard_map.111 = bf16[8,72,128]{2,1,0:T(8,128)(2,1)} custom-call(s32[16]{0:T(128)S(1)} %pad_add_fusion.scal, bf16[8,70,320]{2,1,0:T(8,128)(2,1)S(1)} %all-to-all-done.rows), custom_call_target="tpu_custom_call" | custom-call | flops 10000000 | bytes 1048576 | tf_op jit(solution)/shard_map/pallas_call | solution.py:311
  31.2 9.7 %all-to-all-start.1 = ((bf16[8,72,128]{2,1,0:T(8,128)(2,1)}), bf16[8,72,128]{2,1,0:T(8,128)(2,1)S(1)}, u32[]{:S(2)}, u32[]{:S(2)}) async-start(bf16[8,72,128]{2,1,0:T(8,128)(2,1)} %shard_map.111), calls=%async_computation.1 | async-start | bytes 294912 | tf_op jit(solution)/shard_map/all_to_all | solution.py:426
  41.0 1.2 %copy-done.2 = bf16[8,512,128]{2,1,0:T(8,128)(2,1)S(1)} copy-done((bf16[8,512,128]{2,1,0:T(8,128)(2,1)S(1)}, bf16[8,512,128]{2,1,0:T(8,128)(2,1)}, u32[]{:S(2)}) %copy-start.2) | copy-done | bytes 1048600
  42.2 0.9 copy-done.3
  43.2 15.0 %shard_map.112 = (f32[6336,128]{1,0:T(8,128)}, f32[6336,128]{1,0:T(8,128)}, f32[96,256]{1,0:T(8,128)S(1)}, bf16[384,240]{1,0:T(8,128)(2,1)S(1)}, bf16[288,240]{1...) custom-call(s32[11]{0:T(128)S(1)} %stack.51.scal, ...), custom_call_target="tpu_custom_call" | custom-call | flops 6000000000 | bytes 1048576 | tf_op jit(solution)/shard_map/pallas_call | solution.py:311
  58.2 0.7 copy-done.6
  58.9 0.7 copy-done.7
  59.6 0.7 copy-done.8
  60.2 0.7 copy-done.9
  60.9 0.6 copy-done.10
  61.5 0.6 copy-done.11
  62.1 0.6 copy-done.12
  62.9 14.2 %all_to_all.15 = bf16[16,2,72,128]{3,2,1,0:T(8,128)(2,1)S(1)} all-to-all(bf16[16,2,72,128]{3,2,1,0:T(8,128)(2,1)S(1)} %broadcast_in_dim.17), channel_id=1, replica_groups={{0,2,4,6,8,10,12,46,48,50,52,54,56,58,60,62},{1,3,5,7,9,11,13,47,49,51,..., dimensions={0} | all-to-all | bytes 1179648 | tf_op jit(solution)/shard_map/all_to_all | solution.py:426
  77.1 2.0 %collective-permute-done.4.wb = bf16[2304,128]{1,0:T(8,128)(2,1)S(1)} collective-permute-done((bf16[2304,128]{1,0:T(8,128)(2,1)S(1)}, bf16[2304,128]{1,0:T(8,128)(2,1)S(1)}, u32[]{:S(2)}, u32[]{:S(2)}) %collective-permute-start.4) | collective-permute-done | bytes 589856 | tf_op jit(solution)/shard_map/ppermute | solution.py:488
  79.1 0.8 copy-done.18
  79.9 28.5 %shard_map.113 = bf16[96,64,128]{2,1,0:T(8,128)(2,1)} custom-call(s32[11]{0:T(128)} %copy-done, bf16[2304,128]{1,0:T(8,128)(2,1)} %bitcast.40, bf16[2304,128]{1,0:T(8,128)(2,1)} %copy-done.18, bf16[256,128]{1,0:T(8,128)(2,1)} %copy-done.11, bf16[128,64]{1,0:T(8,128)(2,1)} %copy-done.12, bf16[384,240]{1,0:T(8,128)(2,1)} %copy-done.7, ...), custom_call_target="tpu_custom_call" | custom-call | flops 8000000000 | bytes 1048576 | tf_op jit(solution)/shard_map/pallas_call | solution.py:311
  (41 shorter events, 0.5 us)
Async XLA Ops:
  0.0 1.4 %copy-start.1 = (bf16[1,99,64,128]{3,2,1,0:T(8,128)(2,1)S(1)}, bf16[1,99,64,128]{3,2,1,0:T(8,128)(2,1)}, u32[]{:S(2)}) copy-start(bf16[1,99,64,128]{3,2,1,0:T(8,128)(2,1)} %param.12) | copy-start | bytes 4866052
  1.4 9.3 %copy-start.14 = (bf16[70,8,320]{2,1,0:T(8,128)(2,1)S(1)}, bf16[70,8,320]{2,1,0:T(8,128)(2,1)}, u32[]{:S(2)}) copy-start(bf16[70,8,320]{2,1,0:T(8,128)(2,1)} %param.11) | copy-start | bytes 1075204
  3.5 13.4 %copy-start.17 = (s32[8,4]{0,1:T(4,128)S(1)}, s32[8,4]{0,1:T(4,128)}, u32[]{:S(2)}) copy-start(s32[8,4]{0,1:T(4,128)} %param.13) | copy-start | bytes 388
  3.6 14.6 %copy-start.15 = (bf16[3,3,96,169]{2,3,1,0:T(8,128)(2,1)S(1)}, bf16[3,3,96,169]{2,3,1,0:T(8,128)(2,1)}, u32[]{:S(2)}) copy-start(bf16[3,3,96,169]{2,3,1,0:T(8,128)(2,1)} %param.16) | copy-start | bytes 876100
  3.6 14.8 %copy-start.16 = (bf16[2,512,64]{1,2,0:T(8,128)(2,1)S(1)}, bf16[2,512,64]{1,2,0:T(8,128)(2,1)}, u32[]{:S(2)}) copy-start(bf16[2,512,64]{1,2,0:T(8,128)(2,1)} %param.15) | copy-start | bytes 393220
  4.2 18.0 %collective-permute-start = (bf16[224,128]{1,0:T(8,128)(2,1)}, bf16[224,128]{1,0:T(8,128)(2,1)S(1)}, u32[]{:S(2)}, u32[]{:S(2)}) collective-permute-start(bf16[224,128]{1,0:T(8,128)(2,1)} %get-tuple-element.52), channel_id=1, source_target_pairs={{60,0},{61,1},{62,2},{63,3},{0,4},{1,5},{2,6},{3,7},{4,8},{5,9},{6... | collective-permute-start | bytes 172040 | tf_op jit(solution)/shard_map/ppermute | solution.py:433
  7.2 15.0 %collective-permute-start.1 = (bf16[224,128]{1,0:T(8,128)(2,1)S(1)}, bf16[224,128]{1,0:T(8,128)(2,1)S(1)}, u32[]{:S(2)}, u32[]{:S(2)}) collective-permute-start(bf16[224,128]{1,0:T(8,128)(2,1)S(1)} %get-tuple-element.51), channel_id=1, source_target_pairs={{4,0},{5,1},{6,2},{7,3},{8,4},{9,5},{10,6},{11,7},{12,8},{13,9},{1... | collective-permute-start | bytes 172040 | tf_op jit(solution)/shard_map/ppermute | solution.py:433
  11.6 29.4 %copy-start.4 = (f32[96]{0:T(128)S(1)}, f32[96]{0:T(128)}, u32[]{:S(2)}) copy-start(f32[96]{0:T(128)} %param.17) | copy-start | bytes 1156
  11.6 29.4 %copy-start.5 = (f32[96]{0:T(128)S(1)}, f32[96]{0:T(128)}, u32[]{:S(2)}) copy-start(f32[96]{0:T(128)} %param.19) | copy-start | bytes 1156
  11.6 18.1 %all-to-all-start = ((bf16[8,70,320]{2,1,0:T(8,128)(2,1)}), bf16[8,70,320]{2,1,0:T(8,128)(2,1)S(1)}, u32[]{:S(2)}, u32[]{:S(2)}) async-start(bf16[8,70,320]{2,1,0:T(8,128)(2,1)} %bitcast.32), calls=%async_computation | async-start | bytes 884736 | tf_op jit(solution)/shard_map/all_to_all | solution.py:426
  21.5 36.7 %copy-start = (s32[11]{0:T(128)}, s32[11]{0:T(128)S(1)}, u32[]{:S(2)}) copy-start(s32[11]{0:T(128)S(1)} %stack.51.scal) | copy-start | bytes 136
  23.0 18.0 %collective-permute-start.2 = (bf16[224,128]{1,0:T(8,128)(2,1)S(1)}, bf16[224,128]{1,0:T(8,128)(2,1)S(1)}, u32[]{:S(2)}, u32[]{:S(2)}) collective-permute-start(bf16[224,128]{1,0:T(8,128)(2,1)S(1)} %get-tuple-element.54), channel_id=1, source_target_pairs={{63,0},{0,1},{1,2},{2,3},{3,4},{4,5},{5,6},{6,7},{7,8},{8,9},{9,10... | collective-permute-start | bytes 172040 | tf_op jit(solution)/shard_map/ppermute | solution.py:433
  23.1 17.9 %collective-permute-start.3 = (bf16[224,128]{1,0:T(8,128)(2,1)S(1)}, bf16[224,128]{1,0:T(8,128)(2,1)S(1)}, u32[]{:S(2)}, u32[]{:S(2)}) collective-permute-start(bf16[224,128]{1,0:T(8,128)(2,1)S(1)} %get-tuple-element.53), channel_id=1, source_target_pairs={{1,0},{2,1},{3,2},{4,3},{5,4},{6,5},{7,6},{8,7},{9,8},{10,9},{11,1... | collective-permute-start | bytes 172040 | tf_op jit(solution)/shard_map/ppermute | solution.py:433
  31.2 31.5 %all-to-all-start.1 = ((bf16[8,72,128]{2,1,0:T(8,128)(2,1)}), bf16[8,72,128]{2,1,0:T(8,128)(2,1)S(1)}, u32[]{:S(2)}, u32[]{:S(2)}) async-start(bf16[8,72,128]{2,1,0:T(8,128)(2,1)} %shard_map.111), calls=%async_computation.1 | async-start | bytes 294912 | tf_op jit(solution)/shard_map/all_to_all | solution.py:426
  41.0 1.2 %copy-start.2 = (bf16[8,512,128]{2,1,0:T(8,128)(2,1)S(1)}, bf16[8,512,128]{2,1,0:T(8,128)(2,1)}, u32[]{:S(2)}) copy-start(bf16[8,512,128]{2,1,0:T(8,128)(2,1)} %lon.1) | copy-start | bytes 3145732
  42.2 0.9 copy-start.3
  58.2 0.7 copy-start.6
  58.9 0.7 copy-start.7
  59.6 0.7 copy-start.8
  60.2 0.7 copy-start.9
  60.9 0.6 copy-start.10
  61.5 0.6 copy-start.11
  62.1 0.6 copy-start.12
  77.1 2.0 %copy-start.13 = (bf16[16,2,72,128]{3,2,1,0:T(8,128)(2,1)}, bf16[16,2,72,128]{3,2,1,0:T(8,128)(2,1)S(1)}, u32[]{:S(2)}) copy-start(bf16[16,2,72,128]{3,2,1,0:T(8,128)(2,1)S(1)} %all_to_all.15) | copy-start | bytes 1769476
  77.1 2.0 %collective-permute-start.4 = (bf16[2304,128]{1,0:T(8,128)(2,1)S(1)}, bf16[2304,128]{1,0:T(8,128)(2,1)S(1)}, u32[]{:S(2)}, u32[]{:S(2)}) collective-permute-start(bf16[2304,128]{1,0:T(8,128)(2,1)S(1)} %bitcast.39), channel_id=1, source_target_pairs={{0,1},{1,0},{2,3},{3,2},{4,5},{5,4},{6,7},{7,6},{8,9},{9,8},{10,11... | collective-permute-start | bytes 1769480 | tf_op jit(solution)/shard_map/ppermute | solution.py:488
  79.1 0.8 copy-start.18
where the time goes:
time: 109 us; the launch traced here: 108 us
  Pallas kernels  47.9 us (44%)
  starting transfers between devices  27.6 us (25%)
  local copies, waits for them, and re-layouts  15.2 us (14%)
  blocking collectives  14.2 us (13%)
  waiting for transfers between devices  2.02 us (2%)
  other arithmetic  1.3 us (1%)
    pallas_call x5, Pallas kernels, call(): pl.pallas_call(body, grid_spec=pltpu.PrefetchScalarGridSpec(num_scalar_pr...  47.9 us
    all_to_all x2, starting transfers between devices, swap(): lax.all_to_all(value, EVERY, split_axis=0, concat_axis=0, axis_index_grou...  15.1 us
    all_to_all x1, blocking collectives, swap(): lax.all_to_all(value, EVERY, split_axis=0, concat_axis=0, axis_index_grou...  14.2 us
    ppermute x4, starting transfers between devices, from_neighbour(): lax.ppermute(block, 'tile', [((i - distance) % size, i) for i in range(si...  12.6 us
    unnamed x42, local copies, waits for them, and re-layouts  11.1 us
  transfers between devices with their start and end apart: 7, of which 1 were waited for; matrix products, arithmetic and copies ran while one was open for 6% of the time, Pallas kernels for 16%

commit v1 on v0

--- a/solution.py
+++ b/solution.py
@@ -62,6 +62,25 @@
 
 def stacked(k3, q, och):
     return jnp.concatenate([k3[p, q * och : (q + 1) * och, :] for p in range(3)], axis=0)
+
+
+def paired(count, mix, end, even, odd):
+    mix(0, even)
+
+    def two(i, _):
+        mix(8 * i + 4, odd)
+        end(8 * i, even)
+        mix(8 * i + 8, even)
+        end(8 * i + 4, odd)
+        return 0
+
+    lax.fori_loop(0, (count - 1) // 2, two, 0)
+    if count % 2 == 0:
+        mix(4 * count - 4, odd)
+        end(4 * count - 8, even)
+        end(4 * count - 4, odd)
+    else:
+        end(4 * count - 4, even)
 
 
 def turn_body(state, xs, strips, flat, packs):
@@ -111,7 +130,7 @@
 def early_body(
     scal, xs_own, above, below, ext, west, east, k1, sw, k2, lon, lat, rho, b1, b2,
     acc, skip, side, w1c, v1c, e1c, w2, lonb, latb,
-    xs, w1s, sem,
+    xs, w1s, wide1, wide2, even, odd, sem,
 ):
     och = sw.shape[0]
     cin = sw.shape[1]
@@ -122,6 +141,9 @@
     xs[pl.ds(0, 2 * SP), :] = jnp.where(top, above[...], 0)
     xs[pl.ds(66 * SP, 2 * SP), :] = jnp.where(bottom, below[...], 0)
     bias1, bias2 = column(b1[...]), column(b2[...])
+    wide1[...] = jnp.broadcast_to(bias1, wide1.shape)
+    wide2[...] = jnp.broadcast_to(bias2, wide2.shape)
+    xs[pl.ds(68 * SP, 2 * SP), :] = jnp.zeros((2 * SP, 128), BF16)
 
     row_s, col_s = iota((cin, 3 * SP), 0), iota((cin, 3 * SP), 1)
     row_c, col_c = iota((cin, 3 * CP), 0), iota((cin, 3 * CP), 1)
@@ -172,22 +194,23 @@
     ]
     fetch.wait()
 
-    def conv(i, _):
-        rows = [xs[rows_at(SP * (2 * i + m), 3 * SP, 16), :] for m in range(2)]
-        got = mm(w1s[...], jnp.concatenate(rows, axis=1))
-        for m in range(2):
+    def mix(r, to):
+        rows = [xs[rows_at(SP * (r + m), 3 * SP, 16), :] for m in range(4)]
+        to[...] = mm(w1s[...], jnp.concatenate(rows, axis=1))
+
+    def end(r, got):
+        for m in range(4):
             parts = got[:, 128 * m : 128 * m + 128]
-            at = rows_at(och * (2 * i + m), och, 16)
-            acc[at, :] = across(parts, edges, 2 * i + m, och) + bias1
-            skip[at, :] = parts[3 * och :] + bias2
-        return 0
-
-    lax.fori_loop(0, 33, conv, 0)
+            at = rows_at(och * (r + m), och, 16)
+            acc[at, :] = across(parts, edges, r + m, och) + wide1[...]
+            skip[at, :] = parts[3 * och :] + wide2[...]
+
+    paired(17, mix, end, even, odd)
 
 
 def late_body(
     scal, wa, wb, lonb, latb, w1c, v1c, e1c, w2, k2, side, acc_hbm, skip_hbm,
-    out, bands, sideb, cf, ch, cs, pc, hid, acc, skip, edge1, edge2, of, sems,
+    out, bands, sideb, cf, ch, cs, pc, hid, acc, skip, edge1, edge2, of, even, odd, sems,
 ):
     och = side.shape[0]
     half = wa.shape[0]
@@ -240,6 +263,7 @@
         return 0
 
     lax.fori_loop(0, 68, turn, 0, unroll=4)
+    cs[pl.ds(68 * CP, 2 * CP), :] = jnp.zeros((2 * CP, 128), BF16)
 
     lane = iota((och, 128), 1)
     got = mm(v1c[...], pc[...])
@@ -259,11 +283,16 @@
     for copy in fetch:
         copy.wait()
 
-    def conv1(i, _):
-        r = 2 * i
-        cond = [cs[rows_at(CP * (r + m), 3 * CP, 16), :] for m in range(2)]
-        got = mm(w1c[...], jnp.concatenate(cond, axis=1))
-        for m in range(2):
+    def window(ref, unit, r):
+        return jnp.concatenate(
+            [ref[rows_at(unit * (r + m), 3 * unit, 16), :] for m in range(4)], axis=1
+        )
+
+    def mix1(r, to):
+        to[...] = mm(w1c[...], window(cs, CP, r))
+
+    def end1(r, got):
+        for m in range(4):
             parts = got[:, 128 * m : 128 * m + 128]
             at = rows_at(och * (r + m), och, 16)
             v = across(parts, edge1, r + m, och) + acc[at, :]
@@ -271,20 +300,17 @@
             live = jnp.where(r + m == 0, scal[0], jnp.where(r + m == 65, scal[1], 1))
             hid[at, :] = (v * live.astype(F32)).astype(BF16)
             skip[at, :] = skip[at, :] + parts[3 * och :]
-        return 0
-
-    lax.fori_loop(0, 33, conv1, 0)
-
-    def conv2(j, _):
-        y = 2 * j
-        above = [hid[rows_at(och * (y + m), 3 * och, 16), :] for m in range(2)]
-        got = mm(w2[...], jnp.concatenate(above, axis=1))
-        for m in range(2):
+
+    def mix2(y, to):
+        to[pl.ds(0, 3 * och), :] = mm(w2[...], window(hid, och, y))
+
+    def end2(y, got):
+        for m in range(4):
             v = across(got[:, 128 * m : 128 * m + 128], edge2, y + m, och)
             of[pl.ds(y + m, och, stride=YP), :] = v + skip[rows_at(och * (y + m + 1), och, 16), :]
-        return 0
-
-    lax.fori_loop(0, 32, conv2, 0)
+
+    paired(17, mix1, end1, even, odd)
+    paired(16, mix2, end2, even, odd)
 
     def leave(o, _):
         out[o] = of[rows_at(YP * o, 64, 8), :].astype(BF16)
@@ -347,11 +373,16 @@
     return call(
         early_body,
         [
-            out((66 * och, 128), F32), out((66 * och, 128), F32), out((och, 256), F32),
+            out((68 * och, 128), F32), out((68 * och, 128), F32), out((och, 256), F32),
             out((4 * och, 3 * CP)), out((3 * och, 3 * CP)), out((2, 3 * och, CP)),
             out((3 * och, 3 * och)), out((256, 128)), out((128, 64)),
         ],
-        [pltpu.VMEM((68 * SP, 128), BF16), pltpu.VMEM((4 * och, 3 * SP), BF16), pltpu.SemaphoreType.DMA],
+        [
+            pltpu.VMEM((70 * SP, 128), BF16), pltpu.VMEM((4 * och, 3 * SP), BF16),
+            pltpu.VMEM((och, 128), F32), pltpu.VMEM((och, 128), F32),
+            pltpu.VMEM((4 * och, 512), F32), pltpu.VMEM((4 * och, 512), F32),
+            pltpu.SemaphoreType.DMA,
+        ],
         [
             scal, xs, above, below, ext, west, east, k1.reshape(3, 3 * och, cin), sw,
             k2.reshape(3, 3 * och, och), lon, lat, rho, b1[None], b2[None],
@@ -373,16 +404,16 @@
         late_body, [out((och, 64, 128))],
         [
             vm((64 * WP, 128), F32), vm((64 * WP, 128), F32), vm((WP * YP, 128), F32),
-            vm((128 * CP // 16, 128), F32), vm((68 * CP, 128), BF16), vm((3 * CP, 256), BF16),
-            vm((66 * och, 128), BF16), vm((66 * och, 128), F32), vm((66 * och, 128), F32),
+            vm((128 * CP // 16, 128), F32), vm((70 * CP, 128), BF16), vm((3 * CP, 256), BF16),
+            vm((68 * och, 128), BF16), vm((68 * och, 128), F32), vm((68 * och, 128), F32),
             vm((2, och, 128), F32), vm((2, och, 128), F32), vm((och * YP, 128), F32),
-            pltpu.SemaphoreType.DMA((2,)),
+            vm((4 * och, 512), F32), vm((4 * och, 512), F32), pltpu.SemaphoreType.DMA((2,)),
         ],
         [
             scal, wa, wb, lonb, latb, w1c, v1c, e1c, w2, k2.reshape(3, 3 * och, och), side, acc, skip,
         ],
         specs={10: pl.BlockSpec(memory_space=pltpu.HBM), 11: pl.BlockSpec(memory_space=pltpu.HBM)},
-        scalars=1, flops=8 * 10**9, vmem=58,
+        scalars=1, flops=8 * 10**9, vmem=40,
     )[0]
 
 
@@ -466,22 +497,24 @@
     xs, strips = turned_state(regional_state[0])
     above = from_neighbour(xs[-2 * SP :], TCOLS)
     below = from_neighbour(xs[: 2 * SP], -TCOLS)
-    ext = with_corners(scal, strips, above, below)
     residue = ROWS * (tile % ROWS) + tile // ROWS
     source = (windows[:, 0] + (residue - windows[:, 0]) % 64) // 64
     offset = windows[:, 2] - global_field.shape[2] * region
-    where, ext = lax.optimization_barrier((jnp.concatenate([source, offset]), ext))
+    where, above, below = lax.optimization_barrier(
+        (jnp.concatenate([source, offset]), above, below)
+    )
     chosen_parts = picked(where, by_rows)
+    ext = with_corners(scal, strips, above, below)
     west = from_neighbour(ext[: 2 * SP], 1)
     east = from_neighbour(ext[2 * SP :], -1)
+    mixed = swap(chosen_parts, by_domain)
+    piece = mixed.reshape(regions, 2, *mixed.shape[1:]).astype(jnp.float32).sum(0)
+    piece = piece.astype(jnp.bfloat16)
+    piece, west, east = lax.optimization_barrier((piece, west, east))
     parts = early(
         scal, xs, above, below, ext, west, east, first_kernel, shortcut_weight, second_kernel,
         longitude_weights, latitude_weights, rho, first_bias, later_conv_bias,
     )
-    mixed = swap(chosen_parts, by_domain)
-    piece = mixed.reshape(regions, 2, *mixed.shape[1:]).astype(jnp.float32).sum(0)
-    piece = piece.astype(jnp.bfloat16)
-    piece, parts = lax.optimization_barrier((piece, parts))
     sharers = len(spread[0])
     mine = swap(jnp.broadcast_to(piece[None], (sharers, *piece.shape)), spread)
     mine = mine.reshape(-1, piece.shape[-1])

time: 109 us -> 103 us (0.945)
  the two profiles are of different devices: /device:TPU:32 before, /device:TPU:1 now
where the time goes in v1:
time: 103 us
  starting transfers between devices  33.2 us (32%)
  Pallas kernels  32.8 us (32%)
  waiting for transfers between devices  20.4 us (20%)
  local copies, waits for them, and re-layouts  15.7 us (15%)
    pallas_call x5, Pallas kernels, call(): pl.pallas_call(body, grid_spec=pltpu.PrefetchScalarGridSpec(num_scalar_pr...  32.8 us
    all_to_all x3, starting transfers between devices, swap(): lax.all_to_all(value, EVERY, split_axis=0, concat_axis=0, axis_index_grou...  20.5 us
    all_to_all x3, waiting for transfers between devices, swap(): lax.all_to_all(value, EVERY, split_axis=0, concat_axis=0, axis_index_grou...  20.4 us
    unnamed x22, local copies, waits for them, and re-layouts  11.5 us
    ppermute x4, starting transfers between devices, from_neighbour(): lax.ppermute(block, 'tile', [((i - distance) % size, i) for i in range(si...  11.1 us
  transfers between devices with their start and end apart: 8, of which 3 were waited for; matrix products, arithmetic and copies ran while one was open for 7% of the time, Pallas kernels for 11%

profile of v1, /device:TPU:1, one launch (start us, length us, event | category | flops | bytes accessed | tf_op | source)
XLA Modules:
  0.0 102.5 jit_solution(6335549475824962278)
XLA Ops:
  0.0 1.4 %copy-done = bf16[1,99,64,128]{3,2,1,0:T(8,128)(2,1)S(1)} copy-done((bf16[1,99,64,128]{3,2,1,0:T(8,128)(2,1)S(1)}, bf16[1,99,64,128]{3,2,1,0:T(8,128)(2,1)}, u32[]{:S(2)}) %copy-start) | copy-done | bytes 1622040
  1.4 2.1 %shard_map.109 = (bf16[7168,128]{1,0:T(8,128)(2,1)S(1)}, bf16[448,128]{1,0:T(8,128)(2,1)S(1)}) custom-call(bf16[99,64,128]{2,1,0:T(8,128)(2,1)S(1)} %bitcast.36), custom_call_target="tpu_custom_call" | custom-call | flops 1000000000 | bytes 1048576 | tf_op jit(solution)/shard_map/pallas_call | solution.py:337
  3.5 0.0 copy-start.8
  3.6 3.6 %collective-permute-start = (bf16[224,128]{1,0:T(8,128)(2,1)S(1)}, bf16[224,128]{1,0:T(8,128)(2,1)S(1)}, u32[]{:S(2)}, u32[]{:S(2)}) collective-permute-start(bf16[224,128]{1,0:T(8,128)(2,1)S(1)} %get-tuple-element.40), channel_id=1, source_target_pairs={{60,0},{61,1},{62,2},{63,3},{0,4},{1,5},{2,6},{3,7},{4,8},{5,9},{6... | collective-permute-start | bytes 172040 | tf_op jit(solution)/shard_map/ppermute | solution.py:464
  7.2 3.9 %collective-permute-start.1 = (bf16[224,128]{1,0:T(8,128)(2,1)S(1)}, bf16[224,128]{1,0:T(8,128)(2,1)S(1)}, u32[]{:S(2)}, u32[]{:S(2)}) collective-permute-start(bf16[224,128]{1,0:T(8,128)(2,1)S(1)} %get-tuple-element.39), channel_id=1, source_target_pairs={{4,0},{5,1},{6,2},{7,3},{8,4},{9,5},{10,6},{11,7},{12,8},{13,9},{1... | collective-permute-start | bytes 172040 | tf_op jit(solution)/shard_map/ppermute | solution.py:464
  11.1 0.8 copy.17
  11.9 3.5 %all-to-all-start = ((bf16[8,70,320]{2,1,0:T(8,128)(2,1)}), bf16[8,70,320]{2,1,0:T(8,128)(2,1)S(1)}, u32[]{:S(2)}, u32[]{:S(2)}) async-start(bf16[8,70,320]{2,1,0:T(8,128)(2,1)} %bitcast.32), calls=%async_computation | async-start | bytes 884736 | tf_op jit(solution)/shard_map/all_to_all | solution.py:457
  15.5 0.1 constant_dynamic-slice_fusion
  15.6 0.6 fusion.4
  16.2 1.9 %stack.51.scal = s32[11]{0:T(128)S(1)} concatenate(s32[1]{0:T(128)} %bitcast, s32[1]{0:T(128)} %bitcast.1, s32[1]{0:T(128)} %bitcast.2, s32[1]{0:T(128)} %bitcast.3, s32[1]{0:T(128)} %bitcast.4, s32[1]{0:T(128)} %bitcast.5, s32[1]{0:T(128)} %bitcast.6, s32[1]{0:T(128)} %bitcast.7, s32[1]{0:T(128)} %bitcast.8, s32[1]{0:T(128)} %bitcast.9, s32[1]{0:T(128)} %bitcast.10), dimensions={0} | concatenate | bytes 88 | tf_op jit(solution)/shard_map/stack | solution.py:494
  18.2 0.1 pad_add_fusion.scal
  18.3 0.7 shard_map.111.ext
  19.0 3.1 %all-to-all-done.rows = bf16[8,70,320]{2,1,0:T(8,128)(2,1)S(1)} async-done(((bf16[8,70,320]{2,1,0:T(8,128)(2,1)}), bf16[8,70,320]{2,1,0:T(8,128)(2,1)S(1)}, u32[]{:S(2)}, u32[]{:S(2)}) %all-to-all-start) | async-done | bytes 358432 | tf_op jit(solution)/shard_map/all_to_all | solution.py:457
  22.1 1.5 %shard_map.110 = bf16[8,72,128]{2,1,0:T(8,128)(2,1)} custom-call(s32[16]{0:T(128)S(1)} %pad_add_fusion.scal, bf16[8,70,320]{2,1,0:T(8,128)(2,1)S(1)} %all-to-all-done.rows), custom_call_target="tpu_custom_call" | custom-call | flops 10000000 | bytes 1048576 | tf_op jit(solution)/shard_map/pallas_call | solution.py:337
  23.7 9.1 %all-to-all-start.1 = ((bf16[8,72,128]{2,1,0:T(8,128)(2,1)}), bf16[8,72,128]{2,1,0:T(8,128)(2,1)S(1)}, u32[]{:S(2)}, u32[]{:S(2)}) async-start(bf16[8,72,128]{2,1,0:T(8,128)(2,1)} %shard_map.110), calls=%async_computation.1 | async-start | bytes 294912 | tf_op jit(solution)/shard_map/all_to_all | solution.py:457
  32.8 0.0 copy-start.4
  32.8 3.5 %collective-permute-start.2 = (bf16[224,128]{1,0:T(8,128)(2,1)S(1)}, bf16[224,128]{1,0:T(8,128)(2,1)S(1)}, u32[]{:S(2)}, u32[]{:S(2)}) collective-permute-start(bf16[224,128]{1,0:T(8,128)(2,1)S(1)} %get-tuple-element.42), channel_id=1, source_target_pairs={{63,0},{0,1},{1,2},{2,3},{3,4},{4,5},{5,6},{6,7},{7,8},{8,9},{9,10... | collective-permute-start | bytes 172040 | tf_op jit(solution)/shard_map/ppermute | solution.py:464
  36.3 5.7 %all-to-all-done.1 = bf16[8,72,128]{2,1,0:T(8,128)(2,1)S(1)} async-done(((bf16[8,72,128]{2,1,0:T(8,128)(2,1)}), bf16[8,72,128]{2,1,0:T(8,128)(2,1)S(1)}, u32[]{:S(2)}, u32[]{:S(2)}) %all-to-all-start.1) | async-done | bytes 147488 | tf_op jit(solution)/shard_map/all_to_all | solution.py:457
  42.0 0.9 broadcast_in_dim.15
  42.9 8.0 %all-to-all-start.2 = ((bf16[16,2,72,128]{3,2,1,0:T(8,128)(2,1)}), bf16[16,2,72,128]{3,2,1,0:T(8,128)(2,1)S(1)}, u32[]{:S(2)}, u32[]{:S(2)}) async-start(bf16[16,2,72,128]{3,2,1,0:T(8,128)(2,1)} %broadcast_in_dim.15), calls=%async_computation.2 | async-start | bytes 1179648 | tf_op jit(solution)/shard_map/all_to_all | solution.py:457
  50.9 11.6 %all-to-all-done.2 = bf16[16,2,72,128]{3,2,1,0:T(8,128)(2,1)S(1)} async-done(((bf16[16,2,72,128]{3,2,1,0:T(8,128)(2,1)}), bf16[16,2,72,128]{3,2,1,0:T(8,128)(2,1)S(1)}, u32[]{:S(2)}, u32[]{:S(2)}) %all-to-all-start.2) | async-done | bytes 589856 | tf_op jit(solution)/shard_map/all_to_all | solution.py:457
  62.5 1.6 %collective-permute-start.4 = (bf16[2304,128]{1,0:T(8,128)(2,1)S(1)}, bf16[2304,128]{1,0:T(8,128)(2,1)}, u32[]{:S(2)}, u32[]{:S(2)}) collective-permute-start(bf16[2304,128]{1,0:T(8,128)(2,1)S(1)} %bitcast.33), channel_id=1, source_target_pairs={{0,1},{1,0},{2,3},{3,2},{4,5},{5,4},{6,7},{7,6},{8,9},{9,8},{10,11... | collective-permute-start | bytes 1769480 | tf_op jit(solution)/shard_map/ppermute | solution.py:521
  64.2 0.7 dynamic-slice_bitcast_fusion.rho
  64.9 1.2 %copy.13 = bf16[3,3,96,169]{3,2,1,0:T(8,128)(2,1)S(1)} copy(bf16[3,3,96,169]{2,3,1,0:T(8,128)(2,1)} %param.16) | data formatting | bytes 584064 | tf_op args[5]
  66.1 1.1 %copy.15.lat = bf16[2,512,64]{2,1,0:T(8,128)(2,1)S(1)} copy(bf16[2,512,64]{1,2,0:T(8,128)(2,1)} %param.15) | data formatting | bytes 262144 | tf_op args[4]
  67.2 0.9 copy.14.sw
  68.1 1.2 %copy-done.1 = bf16[8,512,128]{2,1,0:T(8,128)(2,1)S(1)} copy-done((bf16[8,512,128]{2,1,0:T(8,128)(2,1)S(1)}, bf16[8,512,128]{2,1,0:T(8,128)(2,1)}, u32[]{:S(2)}) %copy-start.1) | copy-done | bytes 1048600
  69.3 0.9 copy-done.2
  70.2 10.3 %shard_map.112 = (f32[6528,128]{1,0:T(8,128)}, f32[6528,128]{1,0:T(8,128)}, f32[96,256]{1,0:T(8,128)S(1)}, bf16[384,240]{1,0:T(8,128)(2,1)S(1)}, bf16[288,240]{1...) custom-call(s32[11]{0:T(128)S(1)} %stack.51.scal, ...), custom_call_target="tpu_custom_call" | custom-call | flops 6000000000 | bytes 1048576 | tf_op jit(solution)/shard_map/pallas_call | solution.py:337
  80.6 1.9 %copy-done.5 = f32[6528,128]{1,0:T(8,128)S(1)} copy-done((f32[6528,128]{1,0:T(8,128)S(1)}, f32[6528,128]{1,0:T(8,128)}, u32[]{:S(2)}) %copy-start.5) | copy-done | bytes 3342360
  82.5 1.9 %copy-done.6 = f32[6528,128]{1,0:T(8,128)S(1)} copy-done((f32[6528,128]{1,0:T(8,128)S(1)}, f32[6528,128]{1,0:T(8,128)}, u32[]{:S(2)}) %copy-start.6) | copy-done | bytes 3342360
  84.5 18.0 %shard_map.113 = bf16[96,64,128]{2,1,0:T(8,128)(2,1)} custom-call(s32[11]{0:T(128)S(1)} %stack.51.scal, bf16[2304,128]{1,0:T(8,128)(2,1)S(1)} %bitcast.34, bf16[2304,128]{1,0:T(8,128)(2,1)} %collective-permute-done.4.wb, bf16[256,128]{1,0:T(8,128)(2,1)S(1)} %get-tuple-element.30.lonb, bf16[128,64]{1,0:T(8,128)(2,1)S(1)} %get-tuple-element.31.latb, ...), custom_call_target="tpu_custom_call" | custom-call | flops 8000000000 | bytes 1048576 | tf_op jit(solution)/shard_map/pallas_call | solution.py:337
  (22 shorter events, 0.1 us)
Async XLA Ops:
  0.0 1.4 %copy-start = (bf16[1,99,64,128]{3,2,1,0:T(8,128)(2,1)S(1)}, bf16[1,99,64,128]{3,2,1,0:T(8,128)(2,1)}, u32[]{:S(2)}) copy-start(bf16[1,99,64,128]{3,2,1,0:T(8,128)(2,1)} %param.12) | copy-start | bytes 4866052
  1.4 9.7 %copy-start.7 = (bf16[70,8,320]{2,1,0:T(8,128)(2,1)S(1)}, bf16[70,8,320]{2,1,0:T(8,128)(2,1)}, u32[]{:S(2)}) copy-start(bf16[70,8,320]{2,1,0:T(8,128)(2,1)} %param.11) | copy-start | bytes 1075204
  3.5 12.0 %copy-start.8 = (s32[8,4]{0,1:T(4,128)S(1)}, s32[8,4]{0,1:T(4,128)}, u32[]{:S(2)}) copy-start(s32[8,4]{0,1:T(4,128)} %param.13) | copy-start | bytes 388
  3.6 14.7 %collective-permute-start = (bf16[224,128]{1,0:T(8,128)(2,1)S(1)}, bf16[224,128]{1,0:T(8,128)(2,1)S(1)}, u32[]{:S(2)}, u32[]{:S(2)}) collective-permute-start(bf16[224,128]{1,0:T(8,128)(2,1)S(1)} %get-tuple-element.40), channel_id=1, source_target_pairs={{60,0},{61,1},{62,2},{63,3},{0,4},{1,5},{2,6},{3,7},{4,8},{5,9},{6... | collective-permute-start | bytes 172040 | tf_op jit(solution)/shard_map/ppermute | solution.py:464
  7.2 11.0 %collective-permute-start.1 = (bf16[224,128]{1,0:T(8,128)(2,1)S(1)}, bf16[224,128]{1,0:T(8,128)(2,1)S(1)}, u32[]{:S(2)}, u32[]{:S(2)}) collective-permute-start(bf16[224,128]{1,0:T(8,128)(2,1)S(1)} %get-tuple-element.39), channel_id=1, source_target_pairs={{4,0},{5,1},{6,2},{7,3},{8,4},{9,5},{10,6},{11,7},{12,8},{13,9},{1... | collective-permute-start | bytes 172040 | tf_op jit(solution)/shard_map/ppermute | solution.py:464
  11.9 10.2 %all-to-all-start = ((bf16[8,70,320]{2,1,0:T(8,128)(2,1)}), bf16[8,70,320]{2,1,0:T(8,128)(2,1)S(1)}, u32[]{:S(2)}, u32[]{:S(2)}) async-start(bf16[8,70,320]{2,1,0:T(8,128)(2,1)} %bitcast.32), calls=%async_computation | async-start | bytes 884736 | tf_op jit(solution)/shard_map/all_to_all | solution.py:457
  23.7 18.3 %all-to-all-start.1 = ((bf16[8,72,128]{2,1,0:T(8,128)(2,1)}), bf16[8,72,128]{2,1,0:T(8,128)(2,1)S(1)}, u32[]{:S(2)}, u32[]{:S(2)}) async-start(bf16[8,72,128]{2,1,0:T(8,128)(2,1)} %shard_map.110), calls=%async_computation.1 | async-start | bytes 294912 | tf_op jit(solution)/shard_map/all_to_all | solution.py:457
  32.7 35.3 %copy-start.3 = (f32[96]{0:T(128)S(1)}, f32[96]{0:T(128)}, u32[]{:S(2)}) copy-start(f32[96]{0:T(128)} %param.17) | copy-start | bytes 1156
  32.8 35.3 %copy-start.4 = (f32[96]{0:T(128)S(1)}, f32[96]{0:T(128)}, u32[]{:S(2)}) copy-start(f32[96]{0:T(128)} %param.19) | copy-start | bytes 1156
  32.8 9.2 %collective-permute-start.2 = (bf16[224,128]{1,0:T(8,128)(2,1)S(1)}, bf16[224,128]{1,0:T(8,128)(2,1)S(1)}, u32[]{:S(2)}, u32[]{:S(2)}) collective-permute-start(bf16[224,128]{1,0:T(8,128)(2,1)S(1)} %get-tuple-element.42), channel_id=1, source_target_pairs={{63,0},{0,1},{1,2},{2,3},{3,4},{4,5},{5,6},{6,7},{7,8},{8,9},{9,10... | collective-permute-start | bytes 172040 | tf_op jit(solution)/shard_map/ppermute | solution.py:464
  36.3 5.7 %collective-permute-start.3 = (bf16[224,128]{1,0:T(8,128)(2,1)S(1)}, bf16[224,128]{1,0:T(8,128)(2,1)S(1)}, u32[]{:S(2)}, u32[]{:S(2)}) collective-permute-start(bf16[224,128]{1,0:T(8,128)(2,1)S(1)} %get-tuple-element.41), channel_id=1, source_target_pairs={{1,0},{2,1},{3,2},{4,3},{5,4},{6,5},{7,6},{8,7},{9,8},{10,9},{11,1... | collective-permute-start | bytes 172040 | tf_op jit(solution)/shard_map/ppermute | solution.py:464
  42.9 19.6 %all-to-all-start.2 = ((bf16[16,2,72,128]{3,2,1,0:T(8,128)(2,1)}), bf16[16,2,72,128]{3,2,1,0:T(8,128)(2,1)S(1)}, u32[]{:S(2)}, u32[]{:S(2)}) async-start(bf16[16,2,72,128]{3,2,1,0:T(8,128)(2,1)} %broadcast_in_dim.15), calls=%async_computation.2 | async-start | bytes 1179648 | tf_op jit(solution)/shard_map/all_to_all | solution.py:457
  62.5 18.0 %collective-permute-start.4 = (bf16[2304,128]{1,0:T(8,128)(2,1)S(1)}, bf16[2304,128]{1,0:T(8,128)(2,1)}, u32[]{:S(2)}, u32[]{:S(2)}) collective-permute-start(bf16[2304,128]{1,0:T(8,128)(2,1)S(1)} %bitcast.33), channel_id=1, source_target_pairs={{0,1},{1,0},{2,3},{3,2},{4,5},{5,4},{6,7},{7,6},{8,9},{9,8},{10,11... | collective-permute-start | bytes 1769480 | tf_op jit(solution)/shard_map/ppermute | solution.py:521
  68.1 1.2 %copy-start.1 = (bf16[8,512,128]{2,1,0:T(8,128)(2,1)S(1)}, bf16[8,512,128]{2,1,0:T(8,128)(2,1)}, u32[]{:S(2)}) copy-start(bf16[8,512,128]{2,1,0:T(8,128)(2,1)} %lon.1) | copy-start | bytes 3145732
  69.3 0.9 copy-start.2
  80.6 1.9 %copy-start.5 = (f32[6528,128]{1,0:T(8,128)S(1)}, f32[6528,128]{1,0:T(8,128)}, u32[]{:S(2)}) copy-start(f32[6528,128]{1,0:T(8,128)} %get-tuple-element.37.acc_hbm) | copy-start | bytes 10027012
  82.5 1.9 %copy-start.6 = (f32[6528,128]{1,0:T(8,128)S(1)}, f32[6528,128]{1,0:T(8,128)}, u32[]{:S(2)}) copy-start(f32[6528,128]{1,0:T(8,128)} %get-tuple-element.38.skip_hbm) | copy-start | bytes 10027012

commit v2 on v1

--- a/solution.py
+++ b/solution.py
@@ -127,24 +127,14 @@
         ext[pl.ds(SP * j, SP), :] = e.astype(BF16)
 
 
-def early_body(
-    scal, xs_own, above, below, ext, west, east, k1, sw, k2, lon, lat, rho, b1, b2,
-    acc, skip, side, w1c, v1c, e1c, w2, lonb, latb,
-    xs, w1s, wide1, wide2, even, odd, sem,
+def pack_body(
+    scal, k1, sw, k2, lon, lat, rho, b1, b2,
+    w1s, v1s, w1c, v1c, e1c, w2, lonb, latb, wide1, wide2,
 ):
-    och = sw.shape[0]
-    cin = sw.shape[1]
+    och, cin = sw.shape
     sch = cin - 70
-    fetch = pltpu.make_async_copy(xs_own, xs.at[pl.ds(2 * SP, 64 * SP)], sem)
-    fetch.start()
-    top, bottom, left, right = scal[0] > 0, scal[1] > 0, scal[2] > 0, scal[3] > 0
-    xs[pl.ds(0, 2 * SP), :] = jnp.where(top, above[...], 0)
-    xs[pl.ds(66 * SP, 2 * SP), :] = jnp.where(bottom, below[...], 0)
-    bias1, bias2 = column(b1[...]), column(b2[...])
-    wide1[...] = jnp.broadcast_to(bias1, wide1.shape)
-    wide2[...] = jnp.broadcast_to(bias2, wide2.shape)
-    xs[pl.ds(68 * SP, 2 * SP), :] = jnp.zeros((2 * SP, 128), BF16)
-
+    wide1[...] = jnp.broadcast_to(column(b1[...]), wide1.shape)
+    wide2[...] = jnp.broadcast_to(column(b2[...]), wide2.shape)
     row_s, col_s = iota((cin, 3 * SP), 0), iota((cin, 3 * SP), 1)
     row_c, col_c = iota((cin, 3 * CP), 0), iota((cin, 3 * CP), 1)
     put_s = [chosen((col_s == SP * p + row_s) & (row_s < sch)) for p in range(3)]
@@ -154,7 +144,7 @@
     w1c[pl.ds(0, 3 * och), :] = sum(mm(k1[p], put_c[p]) for p in range(3)).astype(BF16)
     w1c[pl.ds(3 * och, och), :] = mm(sw[...], put_c[1]).astype(BF16)
     turned = [stacked(k1, q, och) for q in range(3)]
-    v1s = sum(mm(turned[q], put_s[q]) for q in range(3)).astype(BF16)
+    v1s[...] = sum(mm(turned[q], put_s[q]) for q in range(3)).astype(BF16)
     v1c[...] = sum(mm(turned[q], put_c[q]) for q in range(3)).astype(BF16)
     row_e, col_e = iota((cin, CP), 0), iota((cin, CP), 1)
     put_e = chosen((col_e == row_e - sch) & (row_e >= sch))
@@ -176,6 +166,20 @@
     order = chosen((iota((64, 64), 0) == want) & (want < scal[7]))
     latb[...] = mm(taken, order).astype(BF16)
 
+
+def early_body(
+    scal, xs_own, above, below, ext, west, east, k1, w1s, v1s, wide1, wide2,
+    acc, skip, side,
+    xs, even, odd, sem,
+):
+    och = side.shape[0]
+    fetch = pltpu.make_async_copy(xs_own, xs.at[pl.ds(2 * SP, 64 * SP)], sem)
+    fetch.start()
+    top, bottom, left, right = scal[0] > 0, scal[1] > 0, scal[2] > 0, scal[3] > 0
+    xs[pl.ds(0, 2 * SP), :] = jnp.where(top, above[...], 0)
+    xs[pl.ds(66 * SP, 2 * SP), :] = jnp.where(bottom, below[...], 0)
+    xs[pl.ds(68 * SP, 2 * SP), :] = jnp.zeros((2 * SP, 128), BF16)
+
     west_in = jnp.where(left, west[...], 0)
     east_in = jnp.where(right, east[...], 0)
     ps = jnp.concatenate(
@@ -185,12 +189,12 @@
         ],
         axis=1,
     )
-    got = mm(v1s, ps)
+    got = mm(v1s[...], ps)
     for s in range(2):
-        side[:, 128 * s : 128 * s + 128] = along(got[:, 128 * s : 128 * s + 128], och) + bias1
+        side[:, 128 * s : 128 * s + 128] = along(got[:, 128 * s : 128 * s + 128], och) + wide1[...]
     edges = [
-        along(mm(turned[0][:, :SP], west_in[SP:]), och),
-        along(mm(turned[2][:, :SP], east_in[:SP]), och),
+        along(mm(stacked(k1, 0, och)[:, :SP], west_in[SP:]), och),
+        along(mm(stacked(k1, 2, och)[:, :SP], east_in[:SP]), och),
     ]
     fetch.wait()
 
@@ -208,16 +212,25 @@
     paired(17, mix, end, even, odd)
 
 
+def total_body(mixed, out):
+    piece = mixed[0].astype(F32)
+    for z in range(1, mixed.shape[0]):
+        piece = piece + mixed[z].astype(F32)
+    piece = piece.astype(BF16)
+    for n in range(out.shape[0]):
+        out[n] = piece
+
+
 def late_body(
-    scal, wa, wb, lonb, latb, w1c, v1c, e1c, w2, k2, side, acc_hbm, skip_hbm,
-    out, bands, sideb, cf, ch, cs, pc, hid, acc, skip, edge1, edge2, of, even, odd, sems,
+    scal, wa, wb, lonb, latb, w1c, v1c, e1c, w2, k2, side, acc_far, skip_far,
+    out, bands, sideb, cf, ch, cs, pc, hid, acc, skip, more, edge1, edge2, of, even, odd, sems,
 ):
     och = side.shape[0]
     half = wa.shape[0]
     step = 288
     fetch = [
-        pltpu.make_async_copy(acc_hbm, acc, sems.at[0]),
-        pltpu.make_async_copy(skip_hbm, skip, sems.at[1]),
+        pltpu.make_async_copy(acc_far, acc, sems.at[0]),
+        pltpu.make_async_copy(skip_far, skip, sems.at[1]),
     ]
     for copy in fetch:
         copy.start()
@@ -299,7 +312,7 @@
             v = v / (1.0 + jnp.exp(-v))
             live = jnp.where(r + m == 0, scal[0], jnp.where(r + m == 65, scal[1], 1))
             hid[at, :] = (v * live.astype(F32)).astype(BF16)
-            skip[at, :] = skip[at, :] + parts[3 * och :]
+            more[at, :] = skip[at, :] + parts[3 * och :]
 
     def mix2(y, to):
         to[pl.ds(0, 3 * och), :] = mm(w2[...], window(hid, och, y))
@@ -307,7 +320,7 @@
     def end2(y, got):
         for m in range(4):
             v = across(got[:, 128 * m : 128 * m + 128], edge2, y + m, och)
-            of[pl.ds(y + m, och, stride=YP), :] = v + skip[rows_at(och * (y + m + 1), och, 16), :]
+            of[pl.ds(y + m, och, stride=YP), :] = v + more[rows_at(och * (y + m + 1), och, 16), :]
 
     paired(17, mix1, end1, even, odd)
     paired(16, mix2, end2, even, odd)
@@ -327,19 +340,18 @@
         out[d] = jnp.concatenate([got, jnp.zeros((WP - got.shape[0], 128), F32)], axis=0).astype(BF16)
 
 
-def call(body, outs, scratch, args, specs=None, scalars=0, flops=10**7, vmem=48):
+def call(body, outs, scratch, args, specs=None, scalars=0, flops=10**7, vmem=63):
     def whole(shape):
         zeros = (0,) * len(shape)
         return pl.BlockSpec(shape, lambda i, *_: zeros, pipeline_mode=pl.Buffered(1))
 
     specs = specs or {}
-    arrays = args[scalars:]
     return pl.pallas_call(
         body,
         grid_spec=pltpu.PrefetchScalarGridSpec(
             num_scalar_prefetch=scalars,
             grid=(1,),
-            in_specs=[specs.get(n) or whole(a.shape) for n, a in enumerate(arrays)],
+            in_specs=[specs.get(n) or whole(a.shape) for n, a in enumerate(args[scalars:])],
             out_specs=[whole(o.shape) for o in outs],
             scratch_shapes=scratch,
         ),
@@ -357,47 +369,59 @@
     return call(
         turn_body, [out((64 * SP, 128)), out((4 * SP, 128))],
         [pltpu.VMEM((YP * SP, 128), F32), pltpu.VMEM((512, 128), F32)],
-        [state], flops=10**9,
+        [state], flops=10**9, vmem=24,
     )
 
 
 def with_corners(scal, strips, above, below):
     return call(
         corner_body, [out((4 * SP, 128))], [], [scal, strips, above, below],
-        scalars=1,
+        scalars=1, vmem=24,
     )[0]
 
 
-def early(scal, xs, above, below, ext, west, east, k1, sw, k2, lon, lat, rho, b1, b2):
+def packed_weights(scal, k1, sw, k2, lon, lat, rho, b1, b2):
     och, cin = sw.shape
     return call(
+        pack_body,
+        [
+            out((4 * och, 3 * SP)), out((3 * och, 3 * SP)), out((4 * och, 3 * CP)),
+            out((3 * och, 3 * CP)), out((2, 3 * och, CP)), out((3 * och, 3 * och)),
+            out((256, 128)), out((128, 64)), out((och, 128), F32), out((och, 128), F32),
+        ],
+        [],
+        [
+            scal, k1.reshape(3, 3 * och, cin), sw, k2.reshape(3, 3 * och, och), lon, lat, rho,
+            b1[None], b2[None],
+        ],
+        specs={
+            3: pl.BlockSpec((1, 512, 128), lambda i, s: (s[9], 0, 0)),
+            4: pl.BlockSpec((1, 512, 64), lambda i, s: (s[10], 0, 0)),
+        },
+        scalars=1, flops=10**9,
+    )
+
+
+def early(scal, xs, above, below, ext, west, east, k1, w1s, v1s, wide1, wide2):
+    och = k1.shape[2]
+    return call(
         early_body,
-        [
-            out((68 * och, 128), F32), out((68 * och, 128), F32), out((och, 256), F32),
-            out((4 * och, 3 * CP)), out((3 * och, 3 * CP)), out((2, 3 * och, CP)),
-            out((3 * och, 3 * och)), out((256, 128)), out((128, 64)),
-        ],
-        [
-            pltpu.VMEM((70 * SP, 128), BF16), pltpu.VMEM((4 * och, 3 * SP), BF16),
-            pltpu.VMEM((och, 128), F32), pltpu.VMEM((och, 128), F32),
-            pltpu.VMEM((4 * och, 512), F32), pltpu.VMEM((4 * och, 512), F32),
-            pltpu.SemaphoreType.DMA,
-        ],
-        [
-            scal, xs, above, below, ext, west, east, k1.reshape(3, 3 * och, cin), sw,
-            k2.reshape(3, 3 * och, och), lon, lat, rho, b1[None], b2[None],
-        ],
-        specs={
-            0: pl.BlockSpec(memory_space=pltpu.HBM),
-            9: pl.BlockSpec((1, 512, 128), lambda i, s: (s[9], 0, 0)),
-            10: pl.BlockSpec((1, 512, 64), lambda i, s: (s[10], 0, 0)),
-        },
-        scalars=1, flops=6 * 10**9,
-    )
-
-
-def late(scal, wa, wb, k2, parts):
-    acc, skip, side, w1c, v1c, e1c, w2, lonb, latb = parts
+        [out((68 * och, 128), F32), out((68 * och, 128), F32), out((och, 256), F32)],
+        [
+            pltpu.VMEM((70 * SP, 128), BF16), pltpu.VMEM((4 * och, 512), F32),
+            pltpu.VMEM((4 * och, 512), F32), pltpu.SemaphoreType.DMA,
+        ],
+        [
+            scal, xs, above, below, ext, west, east, k1.reshape(3, 3 * och, -1), w1s, v1s,
+            wide1, wide2,
+        ],
+        specs={0: pl.BlockSpec(memory_space=pltpu.HBM)}, scalars=1, flops=6 * 10**9,
+    )
+
+
+def late(scal, wa, wb, k2, packed, parts):
+    acc, skip, side = parts
+    w1c, v1c, e1c, w2, lonb, latb = packed[2:8]
     och = side.shape[0]
     vm = pltpu.VMEM
     return call(
@@ -406,19 +430,23 @@
             vm((64 * WP, 128), F32), vm((64 * WP, 128), F32), vm((WP * YP, 128), F32),
             vm((128 * CP // 16, 128), F32), vm((70 * CP, 128), BF16), vm((3 * CP, 256), BF16),
             vm((68 * och, 128), BF16), vm((68 * och, 128), F32), vm((68 * och, 128), F32),
-            vm((2, och, 128), F32), vm((2, och, 128), F32), vm((och * YP, 128), F32),
+            vm((68 * och, 128), F32), vm((2, och, 128), F32), vm((2, och, 128), F32), vm((och * YP, 128), F32),
             vm((4 * och, 512), F32), vm((4 * och, 512), F32), pltpu.SemaphoreType.DMA((2,)),
         ],
         [
             scal, wa, wb, lonb, latb, w1c, v1c, e1c, w2, k2.reshape(3, 3 * och, och), side, acc, skip,
         ],
         specs={10: pl.BlockSpec(memory_space=pltpu.HBM), 11: pl.BlockSpec(memory_space=pltpu.HBM)},
-        scalars=1, flops=8 * 10**9, vmem=40,
+        scalars=1, flops=8 * 10**9,
     )[0]
 
 
 def picked(scal, rows):
-    return call(pick_body, [out((8, WP, 128))], [], [scal, rows], scalars=1)[0]
+    return call(pick_body, [out((8, WP, 128))], [], [scal, rows], scalars=1, vmem=24)[0]
+
+
+def totals(mixed, copies):
+    return call(total_body, [out((copies, *mixed.shape[1:]))], [], [mixed], vmem=24)[0]
 
 
 def domain_half(tile, tiles, rotation):
@@ -507,19 +535,22 @@
     ext = with_corners(scal, strips, above, below)
     west = from_neighbour(ext[: 2 * SP], 1)
     east = from_neighbour(ext[2 * SP :], -1)
+    packed = packed_weights(
+        scal, first_kernel, shortcut_weight, second_kernel, longitude_weights,
+        latitude_weights, rho, first_bias, later_conv_bias,
+    )
     mixed = swap(chosen_parts, by_domain)
-    piece = mixed.reshape(regions, 2, *mixed.shape[1:]).astype(jnp.float32).sum(0)
-    piece = piece.astype(jnp.bfloat16)
-    piece, west, east = lax.optimization_barrier((piece, west, east))
+    mixed = mixed.reshape(regions, 2, *mixed.shape[1:])
+    mixed, west, east, packed = lax.optimization_barrier((mixed, west, east, packed))
     parts = early(
-        scal, xs, above, below, ext, west, east, first_kernel, shortcut_weight, second_kernel,
-        longitude_weights, latitude_weights, rho, first_bias, later_conv_bias,
-    )
-    sharers = len(spread[0])
-    mine = swap(jnp.broadcast_to(piece[None], (sharers, *piece.shape)), spread)
-    mine = mine.reshape(-1, piece.shape[-1])
+        scal, xs, above, below, ext, west, east, first_kernel, packed[0], packed[1],
+        packed[8], packed[9],
+    )
+    copies = totals(mixed, len(spread[0]))
+    mine = swap(copies, spread)
+    mine = mine.reshape(-1, copies.shape[-1])
     other = lax.ppermute(mine, EVERY, [(i, i ^ 1) for i in range(regions * tile_count)])
-    return late(scal, mine, other, second_kernel, parts)[None]
+    return late(scal, mine, other, second_kernel, packed, parts)[None]
 
 
 def solution(mesh):

time: 103 us -> 94.9 us (0.921)
  blocking collectives: 0 us -> 19.5 us
  waiting for transfers between devices: 20.4 us -> 3.39 us
  starting transfers between devices: 33.2 us -> 24.3 us
  local copies, waits for them, and re-layouts: 15.7 us -> 8.89 us
  Pallas kernels: 32.8 us -> 37.8 us
    all_to_all x0 -> x1, blocking collectives: none -> 19.5 us  [swap(): lax.all_to_all(value, EVERY, split_axis=0, concat_axis=0, axis_index_grou...]
    all_to_all x3 -> x2, waiting for transfers between devices: 20.4 us -> 3.38 us  [swap(): lax.all_to_all(value, EVERY, split_axis=0, concat_axis=0, axis_index_grou...]
    all_to_all x3 -> x2, starting transfers between devices: 20.5 us -> 13.2 us  [swap(): lax.all_to_all(value, EVERY, split_axis=0, concat_axis=0, axis_index_grou...]
    unnamed x22 -> x32, local copies, waits for them, and re-layouts: 11.5 us -> 4.88 us
    pallas_call x5 -> x7, Pallas kernels: 32.8 us -> 37.8 us  [call(): pl.pallas_call(body, grid_spec=pltpu.PrefetchScalarGridSpec(num_scalar_pr...]
    ppermute x1, starting transfers between devices: 1.63 us -> 0.39 us  [shards(): lax.ppermute(mine, EVERY, [(i, i ^ 1) for i in range(regions * tile_count)])]
  transfers between devices with their start and end apart: 8 -> 7, of which waited for: 3 -> 1; matrix products, arithmetic and copies ran while one was open for 7% -> 8% of each run, Pallas kernels for 11% -> 17%
where the time goes in v2:
time: 94.9 us; the launch traced here: 94.4 us
  Pallas kernels  37.8 us (40%)
  starting transfers between devices  24.3 us (26%)
  blocking collectives  19.5 us (21%)
  local copies, waits for them, and re-layouts  8.89 us (9%)
  waiting for transfers between devices  3.39 us (4%)
    pallas_call x7, Pallas kernels, call(): pl.pallas_call(body, grid_spec=pltpu.PrefetchScalarGridSpec(num_scalar_pr...  37.8 us
    all_to_all x1, blocking collectives, swap(): lax.all_to_all(value, EVERY, split_axis=0, concat_axis=0, axis_index_grou...  19.5 us
    all_to_all x2, starting transfers between devices, swap(): lax.all_to_all(value, EVERY, split_axis=0, concat_axis=0, axis_index_grou...  13.2 us
    ppermute x4, starting transfers between devices, from_neighbour(): lax.ppermute(block, 'tile', [((i - distance) % size, i) for i in range(si...  10.7 us
    unnamed x32, local copies, waits for them, and re-layouts  4.88 us
    all_to_all x2, waiting for transfers between devices, swap(): lax.all_to_all(value, EVERY, split_axis=0, concat_axis=0, axis_index_grou...  3.38 us
    another operation x1, local copies, waits for them, and re-layouts, shards(): jnp.stack([*flags, row, col, own[0], own[1], own[3], domain, half])  2.05 us
  transfers between devices with their start and end apart: 7, of which 1 were waited for; matrix products, arithmetic and copies ran while one was open for 8% of the time, Pallas kernels for 17%

profile of v2, /device:TPU:1, one launch (start us, length us, event | category | flops | bytes accessed | tf_op | source)
XLA Modules:
  0.0 94.4 jit_solution(3093122512463187530)
XLA Ops:
  0.0 1.4 %copy-done.5 = bf16[1,99,64,128]{3,2,1,0:T(8,128)(2,1)S(1)} copy-done((bf16[1,99,64,128]{3,2,1,0:T(8,128)(2,1)S(1)}, bf16[1,99,64,128]{3,2,1,0:T(8,128)(2,1)}, u32[]{:S(2)}) %copy-start.5) | copy-done | bytes 1622040
  1.4 2.1 %shard_map.109 = (bf16[7168,128]{1,0:T(8,128)(2,1)S(1)}, bf16[448,128]{1,0:T(8,128)(2,1)S(1)}) custom-call(bf16[99,64,128]{2,1,0:T(8,128)(2,1)S(1)} %bitcast.34), custom_call_target="tpu_custom_call" | custom-call | flops 1000000000 | bytes 1048576 | tf_op jit(solution)/shard_map/pallas_call | solution.py:349
  3.6 0.0 copy-start.11
  3.6 0.0 copy-start.8
  3.6 0.0 copy-start.9
  3.6 0.0 copy-start.10
  3.6 3.6 %collective-permute-start = (bf16[224,128]{1,0:T(8,128)(2,1)S(1)}, bf16[224,128]{1,0:T(8,128)(2,1)S(1)}, u32[]{:S(2)}, u32[]{:S(2)}) collective-permute-start(bf16[224,128]{1,0:T(8,128)(2,1)S(1)} %get-tuple-element.68), channel_id=1, source_target_pairs={{60,0},{61,1},{62,2},{63,3},{0,4},{1,5},{2,6},{3,7},{4,8},{5,9},{6... | collective-permute-start | bytes 172040 | tf_op jit(solution)/shard_map/ppermute | solution.py:492
  7.3 5.0 %collective-permute-start.1 = (bf16[224,128]{1,0:T(8,128)(2,1)S(1)}, bf16[224,128]{1,0:T(8,128)(2,1)S(1)}, u32[]{:S(2)}, u32[]{:S(2)}) collective-permute-start(bf16[224,128]{1,0:T(8,128)(2,1)S(1)} %get-tuple-element.67), channel_id=1, source_target_pairs={{4,0},{5,1},{6,2},{7,3},{8,4},{9,5},{10,6},{11,7},{12,8},{13,9},{1... | collective-permute-start | bytes 172040 | tf_op jit(solution)/shard_map/ppermute | solution.py:492
  12.3 0.8 copy.17
  13.1 3.5 %all-to-all-start = ((bf16[8,70,320]{2,1,0:T(8,128)(2,1)}), bf16[8,70,320]{2,1,0:T(8,128)(2,1)S(1)}, u32[]{:S(2)}, u32[]{:S(2)}) async-start(bf16[8,70,320]{2,1,0:T(8,128)(2,1)} %bitcast.32), calls=%async_computation | async-start | bytes 884736 | tf_op jit(solution)/shard_map/all_to_all | solution.py:485
  16.7 0.1 constant_dynamic-slice_fusion
  16.8 0.6 fusion.4
  17.4 1.0 %copy.13 = bf16[3,3,96,169]{3,2,1,0:T(8,128)(2,1)} copy(bf16[3,3,96,169]{2,3,1,0:T(8,128)(2,1)S(1)} %copy-done.8) | data formatting | bytes 584064 | tf_op args[5]
  18.4 0.9 copy.15.lat
  19.2 0.7 copy.14.sw
  19.9 2.1 %stack.51.scal = s32[11]{0:T(128)S(1)} concatenate(s32[1]{0:T(128)} %bitcast, s32[1]{0:T(128)} %bitcast.1, s32[1]{0:T(128)} %bitcast.2, s32[1]{0:T(128)} %bitcast.3, s32[1]{0:T(128)} %bitcast.4, s32[1]{0:T(128)} %bitcast.5, s32[1]{0:T(128)} %bitcast.6, s32[1]{0:T(128)} %bitcast.7, s32[1]{0:T(128)} %bitcast.8, s32[1]{0:T(128)} %bitcast.9, s32[1]{0:T(128)} %bitcast.10), dimensions={0} | concatenate | bytes 88 | tf_op jit(solution)/shard_map/stack | solution.py:522
  22.0 0.1 pad_add_fusion.scal
  22.1 1.3 %dynamic-slice_bitcast_fusion.rho = s32[1,64]{1,0:T(1,128)} fusion(s32[2,2,64]{2,1,0:T(2,128)} %constant.122.clone, s32[]{:T(128)S(6)} %select_n.64, s32[]{:T(128)S(6)} %select_n.66), kind=kLoop, calls=%fused_computation.12 | loop fusion | bytes 520 | tf_op jit(solution)/shard_map/squeeze | solution.py:523
  23.4 0.7 shard_map.111.ext
  24.2 0.0 all-to-all-done.rows
  24.2 1.5 %shard_map.110 = bf16[8,72,128]{2,1,0:T(8,128)(2,1)} custom-call(s32[16]{0:T(128)S(1)} %pad_add_fusion.scal, bf16[8,70,320]{2,1,0:T(8,128)(2,1)S(1)} %all-to-all-done.rows), custom_call_target="tpu_custom_call" | custom-call | flops 10000000 | bytes 1048576 | tf_op jit(solution)/shard_map/pallas_call | solution.py:349
  25.7 9.7 %all-to-all-start.1 = ((bf16[8,72,128]{2,1,0:T(8,128)(2,1)}), bf16[8,72,128]{2,1,0:T(8,128)(2,1)S(1)}, u32[]{:S(2)}, u32[]{:S(2)}) async-start(bf16[8,72,128]{2,1,0:T(8,128)(2,1)} %shard_map.110), calls=%async_computation.1 | async-start | bytes 294912 | tf_op jit(solution)/shard_map/all_to_all | solution.py:485
  35.4 2.1 %collective-permute-start.2 = (bf16[224,128]{1,0:T(8,128)(2,1)S(1)}, bf16[224,128]{1,0:T(8,128)(2,1)S(1)}, u32[]{:S(2)}, u32[]{:S(2)}) collective-permute-start(bf16[224,128]{1,0:T(8,128)(2,1)S(1)} %get-tuple-element.70), channel_id=1, source_target_pairs={{63,0},{0,1},{1,2},{2,3},{3,4},{4,5},{5,6},{6,7},{7,8},{8,9},{9,10... | collective-permute-start | bytes 172040 | tf_op jit(solution)/shard_map/ppermute | solution.py:492
  37.6 0.0 collective-permute-start.3
  37.6 3.9 %shard_map.112 = (bf16[384,336]{1,0:T(8,128)(2,1)}, bf16[288,336]{1,0:T(8,128)(2,1)}, bf16[384,240]{1,0:T(8,128)(2,1)}, bf16[288,240]{1,0:T(8,128)(2,1)}, bf16[2...) custom-call(s32[11]{0:T(128)} %copy-done.4, ...), custom_call_target="tpu_custom_call" | custom-call | flops 1000000000 | bytes 1048576 | tf_op jit(solution)/shard_map/pallas_call | solution.py:349
  41.4 0.0 collective-permute-done.2.west
  41.5 0.0 collective-permute-done.3.east
  41.5 3.4 %all-to-all-done.1 = bf16[8,72,128]{2,1,0:T(8,128)(2,1)S(1)} async-done(((bf16[8,72,128]{2,1,0:T(8,128)(2,1)}), bf16[8,72,128]{2,1,0:T(8,128)(2,1)S(1)}, u32[]{:S(2)}, u32[]{:S(2)}) %all-to-all-start.1) | async-done | bytes 147488 | tf_op jit(solution)/shard_map/all_to_all | solution.py:485
  44.9 19.5 %all_to_all.15 = bf16[16,2,72,128]{3,2,1,0:T(8,128)(2,1)S(1)} all-to-all(bf16[16,2,72,128]{3,2,1,0:T(8,128)(2,1)S(1)} %shard_map.113), channel_id=1, replica_groups={{0,2,4,6,8,10,12,46,48,50,52,54,56,58,60,62},{1,3,5,7,9,11,13,47,49,51,..., dimensions={0} | all-to-all | bytes 1179648 | tf_op jit(solution)/shard_map/all_to_all | solution.py:485
  64.4 0.4 collective-permute-start.4
  64.8 11.7 %shard_map.114 = (f32[6528,128]{1,0:T(8,128)}, f32[6528,128]{1,0:T(8,128)}, f32[96,256]{1,0:T(8,128)}) custom-call(s32[11]{0:T(128)} %copy-done.4, bf16[7168,128]{1,0:T(8,128)(2,1)} %copy-done.3, bf16[224,128]{1,0:T(8,128)(2,1)} %copy-done.1, bf16[224,128]{1,0:T(8,128)(2,1)} %copy-done.2, bf16[448,128]{1,0:T(8,128)(2,1)} %copy-done, ...), custom_call_target="tpu_custom_call" | custom-call | flops 6000000000 | bytes 1048576 | tf_op jit(solution)/shard_map/pallas_call | solution.py:349
  76.6 17.8 %shard_map.115 = bf16[96,64,128]{2,1,0:T(8,128)(2,1)} custom-call(s32[11]{0:T(128)} %copy-done.4, bf16[2304,128]{1,0:T(8,128)(2,1)} %bitcast.36, bf16[2304,128]{1,0:T(8,128)(2,1)} %collective-permute-done.4.wb, bf16[256,128]{1,0:T(8,128)(2,1)} %get-tuple-element.52.lonb, bf16[128,64]{1,0:T(8,128)(2,1)} %get-tuple-element.53.latb, ...), custom_call_target="tpu_custom_call" | custom-call | flops 8000000000 | bytes 1048576 | tf_op jit(solution)/shard_map/pallas_call | solution.py:349
  (31 shorter events, 0.1 us)
Async XLA Ops:
  0.0 1.4 %copy-start.5 = (bf16[1,99,64,128]{3,2,1,0:T(8,128)(2,1)S(1)}, bf16[1,99,64,128]{3,2,1,0:T(8,128)(2,1)}, u32[]{:S(2)}) copy-start(bf16[1,99,64,128]{3,2,1,0:T(8,128)(2,1)} %param.12) | copy-start | bytes 4866052
  1.4 10.8 %copy-start.7 = (bf16[70,8,320]{2,1,0:T(8,128)(2,1)S(1)}, bf16[70,8,320]{2,1,0:T(8,128)(2,1)}, u32[]{:S(2)}) copy-start(bf16[70,8,320]{2,1,0:T(8,128)(2,1)} %param.11) | copy-start | bytes 1075204
  3.5 3.7 %copy-start.3 = (bf16[7168,128]{1,0:T(8,128)(2,1)}, bf16[7168,128]{1,0:T(8,128)(2,1)S(1)}, u32[]{:S(2)}) copy-start(bf16[7168,128]{1,0:T(8,128)(2,1)S(1)} %get-tuple-element.36.xs_own) | copy-start | bytes 5505028
  3.6 13.1 %copy-start.11 = (s32[8,4]{0,1:T(4,128)S(1)}, s32[8,4]{0,1:T(4,128)}, u32[]{:S(2)}) copy-start(s32[8,4]{0,1:T(4,128)} %param.13) | copy-start | bytes 388
  3.6 13.8 %copy-start.8 = (bf16[3,3,96,169]{2,3,1,0:T(8,128)(2,1)S(1)}, bf16[3,3,96,169]{2,3,1,0:T(8,128)(2,1)}, u32[]{:S(2)}) copy-start(bf16[3,3,96,169]{2,3,1,0:T(8,128)(2,1)} %param.16) | copy-start | bytes 876100
  3.6 14.8 %copy-start.9 = (bf16[2,512,64]{1,2,0:T(8,128)(2,1)S(1)}, bf16[2,512,64]{1,2,0:T(8,128)(2,1)}, u32[]{:S(2)}) copy-start(bf16[2,512,64]{1,2,0:T(8,128)(2,1)} %param.15) | copy-start | bytes 393220
  3.6 15.6 %copy-start.10 = (bf16[96,169]{0,1:T(8,128)(2,1)S(1)}, bf16[96,169]{0,1:T(8,128)(2,1)}, u32[]{:S(2)}) copy-start(bf16[96,169]{0,1:T(8,128)(2,1)} %param.20) | copy-start | bytes 97348
  3.6 19.8 %collective-permute-start = (bf16[224,128]{1,0:T(8,128)(2,1)S(1)}, bf16[224,128]{1,0:T(8,128)(2,1)S(1)}, u32[]{:S(2)}, u32[]{:S(2)}) collective-permute-start(bf16[224,128]{1,0:T(8,128)(2,1)S(1)} %get-tuple-element.68), channel_id=1, source_target_pairs={{60,0},{61,1},{62,2},{63,3},{0,4},{1,5},{2,6},{3,7},{4,8},{5,9},{6... | collective-permute-start | bytes 172040 | tf_op jit(solution)/shard_map/ppermute | solution.py:492
  7.3 16.1 %collective-permute-start.1 = (bf16[224,128]{1,0:T(8,128)(2,1)S(1)}, bf16[224,128]{1,0:T(8,128)(2,1)S(1)}, u32[]{:S(2)}, u32[]{:S(2)}) collective-permute-start(bf16[224,128]{1,0:T(8,128)(2,1)S(1)} %get-tuple-element.67), channel_id=1, source_target_pairs={{4,0},{5,1},{6,2},{7,3},{8,4},{9,5},{10,6},{11,7},{12,8},{13,9},{1... | collective-permute-start | bytes 172040 | tf_op jit(solution)/shard_map/ppermute | solution.py:492
  13.1 11.1 %all-to-all-start = ((bf16[8,70,320]{2,1,0:T(8,128)(2,1)}), bf16[8,70,320]{2,1,0:T(8,128)(2,1)S(1)}, u32[]{:S(2)}, u32[]{:S(2)}) async-start(bf16[8,70,320]{2,1,0:T(8,128)(2,1)} %bitcast.32), calls=%async_computation | async-start | bytes 884736 | tf_op jit(solution)/shard_map/all_to_all | solution.py:485
  22.0 15.6 %copy-start.4 = (s32[11]{0:T(128)}, s32[11]{0:T(128)S(1)}, u32[]{:S(2)}) copy-start(s32[11]{0:T(128)S(1)} %stack.51.scal) | copy-start | bytes 136
  23.4 18.0 %copy-start.1 = (bf16[224,128]{1,0:T(8,128)(2,1)}, bf16[224,128]{1,0:T(8,128)(2,1)S(1)}, u32[]{:S(2)}) copy-start(bf16[224,128]{1,0:T(8,128)(2,1)S(1)} %collective-permute-done.above) | copy-start | bytes 172036
  23.4 18.0 %copy-start.2 = (bf16[224,128]{1,0:T(8,128)(2,1)}, bf16[224,128]{1,0:T(8,128)(2,1)S(1)}, u32[]{:S(2)}) copy-start(bf16[224,128]{1,0:T(8,128)(2,1)S(1)} %collective-permute-done.1.below) | copy-start | bytes 172036
  24.1 17.3 %copy-start = (bf16[448,128]{1,0:T(8,128)(2,1)}, bf16[448,128]{1,0:T(8,128)(2,1)S(1)}, u32[]{:S(2)}) copy-start(bf16[448,128]{1,0:T(8,128)(2,1)S(1)} %shard_map.111.ext) | copy-start | bytes 344068
  25.7 19.2 %all-to-all-start.1 = ((bf16[8,72,128]{2,1,0:T(8,128)(2,1)}), bf16[8,72,128]{2,1,0:T(8,128)(2,1)S(1)}, u32[]{:S(2)}, u32[]{:S(2)}) async-start(bf16[8,72,128]{2,1,0:T(8,128)(2,1)} %shard_map.110), calls=%async_computation.1 | async-start | bytes 294912 | tf_op jit(solution)/shard_map/all_to_all | solution.py:485
  35.4 6.0 %collective-permute-start.2 = (bf16[224,128]{1,0:T(8,128)(2,1)S(1)}, bf16[224,128]{1,0:T(8,128)(2,1)S(1)}, u32[]{:S(2)}, u32[]{:S(2)}) collective-permute-start(bf16[224,128]{1,0:T(8,128)(2,1)S(1)} %get-tuple-element.70), channel_id=1, source_target_pairs={{63,0},{0,1},{1,2},{2,3},{3,4},{4,5},{5,6},{6,7},{7,8},{8,9},{9,10... | collective-permute-start | bytes 172040 | tf_op jit(solution)/shard_map/ppermute | solution.py:492
  37.6 3.9 %collective-permute-start.3 = (bf16[224,128]{1,0:T(8,128)(2,1)S(1)}, bf16[224,128]{1,0:T(8,128)(2,1)S(1)}, u32[]{:S(2)}, u32[]{:S(2)}) collective-permute-start(bf16[224,128]{1,0:T(8,128)(2,1)S(1)} %get-tuple-element.69), channel_id=1, source_target_pairs={{1,0},{2,1},{3,2},{4,3},{5,4},{6,5},{7,6},{8,7},{9,8},{10,9},{11,1... | collective-permute-start | bytes 172040 | tf_op jit(solution)/shard_map/ppermute | solution.py:492
  41.5 23.3 %copy-start.12 = (bf16[224,128]{1,0:T(8,128)(2,1)}, bf16[224,128]{1,0:T(8,128)(2,1)S(1)}, u32[]{:S(2)}) copy-start(bf16[224,128]{1,0:T(8,128)(2,1)S(1)} %collective-permute-done.2.west) | copy-start | bytes 172036
  41.5 23.3 %copy-start.13 = (bf16[224,128]{1,0:T(8,128)(2,1)}, bf16[224,128]{1,0:T(8,128)(2,1)S(1)}, u32[]{:S(2)}) copy-start(bf16[224,128]{1,0:T(8,128)(2,1)S(1)} %collective-permute-done.3.east) | copy-start | bytes 172036
  64.4 12.2 %copy-start.6 = (bf16[16,2,72,128]{3,2,1,0:T(8,128)(2,1)}, bf16[16,2,72,128]{3,2,1,0:T(8,128)(2,1)S(1)}, u32[]{:S(2)}) copy-start(bf16[16,2,72,128]{3,2,1,0:T(8,128)(2,1)S(1)} %all_to_all.15) | copy-start | bytes 1769476
  64.4 12.2 %collective-permute-start.4 = (bf16[2304,128]{1,0:T(8,128)(2,1)S(1)}, bf16[2304,128]{1,0:T(8,128)(2,1)}, u32[]{:S(2)}, u32[]{:S(2)}) collective-permute-start(bf16[2304,128]{1,0:T(8,128)(2,1)S(1)} %bitcast.35), channel_id=1, source_target_pairs={{0,1},{1,0},{2,3},{3,2},{4,5},{5,4},{6,7},{7,6},{8,9},{9,8},{10,11... | collective-permute-start | bytes 1769480 | tf_op jit(solution)/shard_map/ppermute | solution.py:552

commit v3 on v2

--- a/solution.py
+++ b/solution.py
@@ -51,36 +51,44 @@
     )
 
 
-def across(parts, edges, at, och):
-    lane = iota((och, 128), 1)
-    west = jnp.where(lane == 0, pltpu.roll(edges[0], 128 - at, 1), pltpu.roll(parts[:och], 1, 1))
-    east = jnp.where(
-        lane == 127, pltpu.roll(edges[1], 127 - at, 1), pltpu.roll(parts[2 * och : 3 * och], 127, 1)
-    )
-    return parts[och : 2 * och] + west + east
+CHUNK = 32
+
+
+def across(parts, m, edges, at, och, k):
+    lanes = pl.ds(128 * m, 128)
+    lane = iota((CHUNK, 128), 1)
+    rows = pl.ds(k, CHUNK)
+    west = pltpu.roll(parts[rows, lanes], 1, 1)
+    east = pltpu.roll(parts[pl.ds(2 * och + k, CHUNK), lanes], 127, 1)
+    west = jnp.where(lane == 0, pltpu.roll(edges[0, rows, :], 128 - at, 1), west)
+    east = jnp.where(lane == 127, pltpu.roll(edges[1, rows, :], 127 - at, 1), east)
+    return parts[pl.ds(och + k, CHUNK), lanes] + west + east
 
 
 def stacked(k3, q, och):
     return jnp.concatenate([k3[p, q * och : (q + 1) * och, :] for p in range(3)], axis=0)
 
 
+def pieces(src, dst, sems, unit):
+    moves = []
+    for g in range(17):
+        at = pl.ds(4 * unit * g, 4 * unit)
+        moves.append(
+            [
+                pltpu.make_async_copy(src[n].at[at, :], dst[n].at[at, :], sems.at[n, g])
+                for n in range(2)
+            ]
+        )
+    return moves
+
+
 def paired(count, mix, end, even, odd):
+    hold = (even, odd)
     mix(0, even)
-
-    def two(i, _):
-        mix(8 * i + 4, odd)
-        end(8 * i, even)
-        mix(8 * i + 8, even)
-        end(8 * i + 4, odd)
-        return 0
-
-    lax.fori_loop(0, (count - 1) // 2, two, 0)
-    if count % 2 == 0:
-        mix(4 * count - 4, odd)
-        end(4 * count - 8, even)
-        end(4 * count - 4, odd)
-    else:
-        end(4 * count - 4, even)
+    for g in range(count):
+        if g + 1 < count:
+            mix(4 * (g + 1), hold[(g + 1) % 2])
+        end(4 * g, hold[g % 2])
 
 
 def turn_body(state, xs, strips, flat, packs):
@@ -169,8 +177,8 @@
 
 def early_body(
     scal, xs_own, above, below, ext, west, east, k1, w1s, v1s, wide1, wide2,
-    acc, skip, side,
-    xs, even, odd, sem,
+    acc_far, skip_far, side,
+    xs, even, odd, edges, acc, skip, sem, sems,
 ):
     och = side.shape[0]
     fetch = pltpu.make_async_copy(xs_own, xs.at[pl.ds(2 * SP, 64 * SP)], sem)
@@ -192,10 +200,8 @@
     got = mm(v1s[...], ps)
     for s in range(2):
         side[:, 128 * s : 128 * s + 128] = along(got[:, 128 * s : 128 * s + 128], och) + wide1[...]
-    edges = [
-        along(mm(stacked(k1, 0, och)[:, :SP], west_in[SP:]), och),
-        along(mm(stacked(k1, 2, och)[:, :SP], east_in[:SP]), och),
-    ]
+    edges[0] = along(mm(stacked(k1, 0, och)[:, :SP], west_in[SP:]), och)
+    edges[1] = along(mm(stacked(k1, 2, och)[:, :SP], east_in[:SP]), och)
     fetch.wait()
 
     def mix(r, to):
@@ -204,12 +210,19 @@
 
     def end(r, got):
         for m in range(4):
-            parts = got[:, 128 * m : 128 * m + 128]
-            at = rows_at(och * (r + m), och, 16)
-            acc[at, :] = across(parts, edges, r + m, och) + wide1[...]
-            skip[at, :] = parts[3 * och :] + wide2[...]
-
+            for k in range(0, och, CHUNK):
+                at = rows_at(och * (r + m) + k, CHUNK, 16)
+                rows = pl.ds(k, CHUNK)
+                acc[at, :] = across(got, m, edges, r + m, och, k) + wide1[rows, :]
+                skip[at, :] = got[pl.ds(3 * och + k, CHUNK), pl.ds(128 * m, 128)] + wide2[rows, :]
+        for copy in moves[r // 4]:
+            copy.start()
+
+    moves = pieces((acc, skip), (acc_far, skip_far), sems, och)
     paired(17, mix, end, even, odd)
+    for pair in moves:
+        for copy in pair:
+            copy.wait()
 
 
 def total_body(mixed, out):
@@ -223,16 +236,16 @@
 
 def late_body(
     scal, wa, wb, lonb, latb, w1c, v1c, e1c, w2, k2, side, acc_far, skip_far,
-    out, bands, sideb, cf, ch, cs, pc, hid, acc, skip, more, edge1, edge2, of, even, odd, sems,
+    out, bands, sideb, cf, ch, cs, pc, hid, acc, skip, more, edge1, edge2, of, even, odd, res, sems, fetched,
 ):
     och = side.shape[0]
     half = wa.shape[0]
     step = 288
-    fetch = [
-        pltpu.make_async_copy(acc_far, acc, sems.at[0]),
-        pltpu.make_async_copy(skip_far, skip, sems.at[1]),
+    moves = [
+        pltpu.make_async_copy(acc_far, acc, fetched.at[0]),
+        pltpu.make_async_copy(skip_far, skip, fetched.at[1]),
     ]
-    for copy in fetch:
+    for copy in moves:
         copy.start()
 
     def spread(k, _):
@@ -293,7 +306,7 @@
         v = jnp.where(keep, v, 0.0).astype(BF16)
         edge2[s] = along(mm(stacked(k2, 2 * s, och), v), och)
         edge1[s] = along(mm(e1c[s], pc[pl.ds(CP, CP), lanes]), och)
-    for copy in fetch:
+    for copy in moves:
         copy.wait()
 
     def window(ref, unit, r):
@@ -306,30 +319,40 @@
 
     def end1(r, got):
         for m in range(4):
-            parts = got[:, 128 * m : 128 * m + 128]
-            at = rows_at(och * (r + m), och, 16)
-            v = across(parts, edge1, r + m, och) + acc[at, :]
-            v = v / (1.0 + jnp.exp(-v))
-            live = jnp.where(r + m == 0, scal[0], jnp.where(r + m == 65, scal[1], 1))
-            hid[at, :] = (v * live.astype(F32)).astype(BF16)
-            more[at, :] = skip[at, :] + parts[3 * och :]
+            live = jnp.where(r + m == 0, scal[0], jnp.where(r + m == 65, scal[1], 1)).astype(F32)
+            for k in range(0, och, CHUNK):
+                at = rows_at(och * (r + m) + k, CHUNK, 16)
+                v = across(got, m, edge1, r + m, och, k) + acc[at, :]
+                v = v / (1.0 + jnp.exp(-v))
+                hid[at, :] = (v * live).astype(BF16)
+                more[at, :] = skip[at, :] + got[pl.ds(3 * och + k, CHUNK), pl.ds(128 * m, 128)]
 
     def mix2(y, to):
         to[pl.ds(0, 3 * och), :] = mm(w2[...], window(hid, och, y))
 
     def end2(y, got):
         for m in range(4):
-            v = across(got[:, 128 * m : 128 * m + 128], edge2, y + m, och)
-            of[pl.ds(y + m, och, stride=YP), :] = v + more[rows_at(och * (y + m + 1), och, 16), :]
-
+            for k in range(0, och, CHUNK):
+                v = across(got, m, edge2, y + m, och, k)
+                v = v + more[rows_at(och * (y + m + 1) + k, CHUNK, 16), :]
+                of[pl.ds(YP * k + y + m, CHUNK, stride=YP), :] = v
+        if y % 16 == 12:
+            at = pl.ds(y - 12, 16)
+            for o in range(och):
+                res[o, at, :] = of[pl.ds(YP * o + y - 12, 16), :].astype(BF16)
+            leaves[y // 16].start()
+
+    leaves = [
+        pltpu.make_async_copy(
+            res.at[:, pl.ds(16 * n, 16), :], out.at[:, pl.ds(16 * n, 16), :], sems.at[n]
+        )
+        for n in range(4)
+    ]
     paired(17, mix1, end1, even, odd)
     paired(16, mix2, end2, even, odd)
 
-    def leave(o, _):
-        out[o] = of[rows_at(YP * o, 64, 8), :].astype(BF16)
-        return 0
-
-    lax.fori_loop(0, och, leave, 0, unroll=4)
+    for copy in leaves:
+        copy.wait()
 
 
 def pick_body(scal, rows, out):
@@ -340,7 +363,7 @@
         out[d] = jnp.concatenate([got, jnp.zeros((WP - got.shape[0], 128), F32)], axis=0).astype(BF16)
 
 
-def call(body, outs, scratch, args, specs=None, scalars=0, flops=10**7, vmem=63):
+def call(body, outs, scratch, args, specs=None, far=(), scalars=0, flops=10**7, vmem=63):
     def whole(shape):
         zeros = (0,) * len(shape)
         return pl.BlockSpec(shape, lambda i, *_: zeros, pipeline_mode=pl.Buffered(1))
@@ -352,7 +375,10 @@
             num_scalar_prefetch=scalars,
             grid=(1,),
             in_specs=[specs.get(n) or whole(a.shape) for n, a in enumerate(args[scalars:])],
-            out_specs=[whole(o.shape) for o in outs],
+            out_specs=[
+                pl.BlockSpec(memory_space=pltpu.HBM) if n in far else whole(o.shape)
+                for n, o in enumerate(outs)
+            ],
             scratch_shapes=scratch,
         ),
         out_shape=outs,
@@ -409,13 +435,15 @@
         [out((68 * och, 128), F32), out((68 * och, 128), F32), out((och, 256), F32)],
         [
             pltpu.VMEM((70 * SP, 128), BF16), pltpu.VMEM((4 * och, 512), F32),
-            pltpu.VMEM((4 * och, 512), F32), pltpu.SemaphoreType.DMA,
+            pltpu.VMEM((4 * och, 512), F32), pltpu.VMEM((2, och, 128), F32),
+            pltpu.VMEM((68 * och, 128), F32), pltpu.VMEM((68 * och, 128), F32),
+            pltpu.SemaphoreType.DMA, pltpu.SemaphoreType.DMA((2, 17)),
         ],
         [
             scal, xs, above, below, ext, west, east, k1.reshape(3, 3 * och, -1), w1s, v1s,
             wide1, wide2,
         ],
-        specs={0: pl.BlockSpec(memory_space=pltpu.HBM)}, scalars=1, flops=6 * 10**9,
+        specs={0: pl.BlockSpec(memory_space=pltpu.HBM)}, far=(0, 1), scalars=1, flops=6 * 10**9,
     )
 
 
@@ -431,13 +459,14 @@
             vm((128 * CP // 16, 128), F32), vm((70 * CP, 128), BF16), vm((3 * CP, 256), BF16),
             vm((68 * och, 128), BF16), vm((68 * och, 128), F32), vm((68 * och, 128), F32),
             vm((68 * och, 128), F32), vm((2, och, 128), F32), vm((2, och, 128), F32), vm((och * YP, 128), F32),
-            vm((4 * och, 512), F32), vm((4 * och, 512), F32), pltpu.SemaphoreType.DMA((2,)),
+            vm((4 * och, 512), F32), vm((4 * och, 512), F32), vm((och, 64, 128), BF16),
+            pltpu.SemaphoreType.DMA((4,)), pltpu.SemaphoreType.DMA((2,)),
         ],
         [
             scal, wa, wb, lonb, latb, w1c, v1c, e1c, w2, k2.reshape(3, 3 * och, och), side, acc, skip,
         ],
         specs={10: pl.BlockSpec(memory_space=pltpu.HBM), 11: pl.BlockSpec(memory_space=pltpu.HBM)},
-        scalars=1, flops=8 * 10**9,
+        far=(0,), scalars=1, flops=8 * 10**9,
     )[0]
 
 

time: 94.9 us -> 89.4 us (0.942)
  Pallas kernels: 37.8 us -> 32.2 us
    pallas_call x7, Pallas kernels: 37.8 us -> 32.2 us  [call(): pl.pallas_call(body, grid_spec=pltpu.PrefetchScalarGridSpec(num_scalar_pr...]
  transfers between devices with their start and end apart: 7 -> 7, of which waited for: 1 -> 1; matrix products, arithmetic and copies ran while one was open for 8% -> 8% of each run, Pallas kernels for 17% -> 15%
where the time goes in v3:
time: 89.4 us; the launch traced here: 88.9 us
  Pallas kernels  32.2 us (36%)
  starting transfers between devices  24.3 us (27%)
  blocking collectives  19.5 us (22%)
  local copies, waits for them, and re-layouts  8.89 us (10%)
  waiting for transfers between devices  3.4 us (4%)
    pallas_call x7, Pallas kernels, call(): pl.pallas_call(body, grid_spec=pltpu.PrefetchScalarGridSpec(num_scalar_pr...  32.2 us
    all_to_all x1, blocking collectives, swap(): lax.all_to_all(value, EVERY, split_axis=0, concat_axis=0, axis_index_grou...  19.5 us
    all_to_all x2, starting transfers between devices, swap(): lax.all_to_all(value, EVERY, split_axis=0, concat_axis=0, axis_index_grou...  13.2 us
    ppermute x4, starting transfers between devices, from_neighbour(): lax.ppermute(block, 'tile', [((i - distance) % size, i) for i in range(si...  10.7 us
    unnamed x32, local copies, waits for them, and re-layouts  4.88 us
    all_to_all x2, waiting for transfers between devices, swap(): lax.all_to_all(value, EVERY, split_axis=0, concat_axis=0, axis_index_grou...  3.38 us
    another operation x1, local copies, waits for them, and re-layouts, shards(): jnp.stack([*flags, row, col, own[0], own[1], own[3], domain, half])  2.05 us
  transfers between devices with their start and end apart: 7, of which 1 were waited for; matrix products, arithmetic and copies ran while one was open for 8% of the time, Pallas kernels for 15%

profile of v3, /device:TPU:1, one launch (start us, length us, event | category | flops | bytes accessed | tf_op | source)
XLA Modules:
  0.0 88.9 jit_solution(6892760578185269686)
XLA Ops:
  0.0 1.4 %copy-done.5 = bf16[1,99,64,128]{3,2,1,0:T(8,128)(2,1)S(1)} copy-done((bf16[1,99,64,128]{3,2,1,0:T(8,128)(2,1)S(1)}, bf16[1,99,64,128]{3,2,1,0:T(8,128)(2,1)}, u32[]{:S(2)}) %copy-start.5) | copy-done | bytes 1622040
  1.4 2.1 %shard_map.109 = (bf16[7168,128]{1,0:T(8,128)(2,1)S(1)}, bf16[448,128]{1,0:T(8,128)(2,1)S(1)}) custom-call(bf16[99,64,128]{2,1,0:T(8,128)(2,1)S(1)} %bitcast.34), custom_call_target="tpu_custom_call" | custom-call | flops 1000000000 | bytes 1048576 | tf_op jit(solution)/shard_map/pallas_call | solution.py:372
  3.6 0.0 copy-start.11
  3.6 0.0 copy-start.8
  3.6 0.0 copy-start.9
  3.6 0.0 copy-start.10
  3.6 3.6 %collective-permute-start = (bf16[224,128]{1,0:T(8,128)(2,1)S(1)}, bf16[224,128]{1,0:T(8,128)(2,1)S(1)}, u32[]{:S(2)}, u32[]{:S(2)}) collective-permute-start(bf16[224,128]{1,0:T(8,128)(2,1)S(1)} %get-tuple-element.68), channel_id=1, source_target_pairs={{60,0},{61,1},{62,2},{63,3},{0,4},{1,5},{2,6},{3,7},{4,8},{5,9},{6... | collective-permute-start | bytes 172040 | tf_op jit(solution)/shard_map/ppermute | solution.py:521
  7.3 5.0 %collective-permute-start.1 = (bf16[224,128]{1,0:T(8,128)(2,1)S(1)}, bf16[224,128]{1,0:T(8,128)(2,1)S(1)}, u32[]{:S(2)}, u32[]{:S(2)}) collective-permute-start(bf16[224,128]{1,0:T(8,128)(2,1)S(1)} %get-tuple-element.67), channel_id=1, source_target_pairs={{4,0},{5,1},{6,2},{7,3},{8,4},{9,5},{10,6},{11,7},{12,8},{13,9},{1... | collective-permute-start | bytes 172040 | tf_op jit(solution)/shard_map/ppermute | solution.py:521
  12.3 0.8 copy.17
  13.1 3.5 %all-to-all-start = ((bf16[8,70,320]{2,1,0:T(8,128)(2,1)}), bf16[8,70,320]{2,1,0:T(8,128)(2,1)S(1)}, u32[]{:S(2)}, u32[]{:S(2)}) async-start(bf16[8,70,320]{2,1,0:T(8,128)(2,1)} %bitcast.32), calls=%async_computation | async-start | bytes 884736 | tf_op jit(solution)/shard_map/all_to_all | solution.py:514
  16.7 0.1 constant_dynamic-slice_fusion
  16.8 0.6 fusion.4
  17.4 1.0 %copy.13 = bf16[3,3,96,169]{3,2,1,0:T(8,128)(2,1)} copy(bf16[3,3,96,169]{2,3,1,0:T(8,128)(2,1)S(1)} %copy-done.8) | data formatting | bytes 584064 | tf_op args[5]
  18.4 0.9 copy.15.lat
  19.2 0.7 copy.14.sw
  19.9 2.1 %stack.51.scal = s32[11]{0:T(128)S(1)} concatenate(s32[1]{0:T(128)} %bitcast, s32[1]{0:T(128)} %bitcast.1, s32[1]{0:T(128)} %bitcast.2, s32[1]{0:T(128)} %bitcast.3, s32[1]{0:T(128)} %bitcast.4, s32[1]{0:T(128)} %bitcast.5, s32[1]{0:T(128)} %bitcast.6, s32[1]{0:T(128)} %bitcast.7, s32[1]{0:T(128)} %bitcast.8, s32[1]{0:T(128)} %bitcast.9, s32[1]{0:T(128)} %bitcast.10), dimensions={0} | concatenate | bytes 88 | tf_op jit(solution)/shard_map/stack | solution.py:551
  22.0 0.1 pad_add_fusion.scal
  22.1 1.3 %dynamic-slice_bitcast_fusion.rho = s32[1,64]{1,0:T(1,128)} fusion(s32[2,2,64]{2,1,0:T(2,128)} %constant.122.clone, s32[]{:T(128)S(6)} %select_n.64, s32[]{:T(128)S(6)} %select_n.66), kind=kLoop, calls=%fused_computation.12 | loop fusion | bytes 520 | tf_op jit(solution)/shard_map/squeeze | solution.py:552
  23.4 0.0 collective-permute-done.above
  23.4 0.7 shard_map.111.ext
  24.2 0.0 all-to-all-done.rows
  24.2 1.5 %shard_map.110 = bf16[8,72,128]{2,1,0:T(8,128)(2,1)} custom-call(s32[16]{0:T(128)S(1)} %pad_add_fusion.scal, bf16[8,70,320]{2,1,0:T(8,128)(2,1)S(1)} %all-to-all-done.rows), custom_call_target="tpu_custom_call" | custom-call | flops 10000000 | bytes 1048576 | tf_op jit(solution)/shard_map/pallas_call | solution.py:372
  25.7 9.7 %all-to-all-start.1 = ((bf16[8,72,128]{2,1,0:T(8,128)(2,1)}), bf16[8,72,128]{2,1,0:T(8,128)(2,1)S(1)}, u32[]{:S(2)}, u32[]{:S(2)}) async-start(bf16[8,72,128]{2,1,0:T(8,128)(2,1)} %shard_map.110), calls=%async_computation.1 | async-start | bytes 294912 | tf_op jit(solution)/shard_map/all_to_all | solution.py:514
  35.4 2.1 %collective-permute-start.2 = (bf16[224,128]{1,0:T(8,128)(2,1)S(1)}, bf16[224,128]{1,0:T(8,128)(2,1)S(1)}, u32[]{:S(2)}, u32[]{:S(2)}) collective-permute-start(bf16[224,128]{1,0:T(8,128)(2,1)S(1)} %get-tuple-element.70), channel_id=1, source_target_pairs={{63,0},{0,1},{1,2},{2,3},{3,4},{4,5},{5,6},{6,7},{7,8},{8,9},{9,10... | collective-permute-start | bytes 172040 | tf_op jit(solution)/shard_map/ppermute | solution.py:521
  37.6 3.9 %shard_map.112 = (bf16[384,336]{1,0:T(8,128)(2,1)}, bf16[288,336]{1,0:T(8,128)(2,1)}, bf16[384,240]{1,0:T(8,128)(2,1)}, bf16[288,240]{1,0:T(8,128)(2,1)}, bf16[2...) custom-call(s32[11]{0:T(128)} %copy-done.4, ...), custom_call_target="tpu_custom_call" | custom-call | flops 1000000000 | bytes 1048576 | tf_op jit(solution)/shard_map/pallas_call | solution.py:372
  41.4 0.0 collective-permute-done.2.west
  41.5 0.0 collective-permute-done.3.east
  41.5 3.4 %all-to-all-done.1 = bf16[8,72,128]{2,1,0:T(8,128)(2,1)S(1)} async-done(((bf16[8,72,128]{2,1,0:T(8,128)(2,1)}), bf16[8,72,128]{2,1,0:T(8,128)(2,1)S(1)}, u32[]{:S(2)}, u32[]{:S(2)}) %all-to-all-start.1) | async-done | bytes 147488 | tf_op jit(solution)/shard_map/all_to_all | solution.py:514
  44.9 19.5 %all_to_all.15 = bf16[16,2,72,128]{3,2,1,0:T(8,128)(2,1)S(1)} all-to-all(bf16[16,2,72,128]{3,2,1,0:T(8,128)(2,1)S(1)} %shard_map.113), channel_id=1, replica_groups={{0,2,4,6,8,10,12,46,48,50,52,54,56,58,60,62},{1,3,5,7,9,11,13,47,49,51,..., dimensions={0} | all-to-all | bytes 1179648 | tf_op jit(solution)/shard_map/all_to_all | solution.py:514
  64.4 0.4 collective-permute-start.4
  64.8 8.9 %shard_map.114 = (f32[6528,128]{1,0:T(8,128)}, f32[6528,128]{1,0:T(8,128)}, f32[96,256]{1,0:T(8,128)}) custom-call(s32[11]{0:T(128)} %copy-done.4, bf16[7168,128]{1,0:T(8,128)(2,1)} %copy-done.3, bf16[224,128]{1,0:T(8,128)(2,1)} %copy-done.1, bf16[224,128]{1,0:T(8,128)(2,1)} %copy-done.2, bf16[448,128]{1,0:T(8,128)(2,1)} %copy-done, ...), custom_call_target="tpu_custom_call" | custom-call | flops 6000000000 | bytes 1048576 | tf_op jit(solution)/shard_map/pallas_call | solution.py:372
  73.8 15.0 %shard_map.115 = bf16[96,64,128]{2,1,0:T(8,128)(2,1)} custom-call(s32[11]{0:T(128)} %copy-done.4, bf16[2304,128]{1,0:T(8,128)(2,1)} %bitcast.36, bf16[2304,128]{1,0:T(8,128)(2,1)} %collective-permute-done.4.wb, bf16[256,128]{1,0:T(8,128)(2,1)} %get-tuple-element.52.lonb, bf16[128,64]{1,0:T(8,128)(2,1)} %get-tuple-element.53.latb, ...), custom_call_target="tpu_custom_call" | custom-call | flops 8000000000 | bytes 1048576 | tf_op jit(solution)/shard_map/pallas_call | solution.py:372
  (31 shorter events, 0.1 us)
Async XLA Ops:
  0.0 1.4 %copy-start.5 = (bf16[1,99,64,128]{3,2,1,0:T(8,128)(2,1)S(1)}, bf16[1,99,64,128]{3,2,1,0:T(8,128)(2,1)}, u32[]{:S(2)}) copy-start(bf16[1,99,64,128]{3,2,1,0:T(8,128)(2,1)} %param.12) | copy-start | bytes 4866052
  1.4 10.8 %copy-start.7 = (bf16[70,8,320]{2,1,0:T(8,128)(2,1)S(1)}, bf16[70,8,320]{2,1,0:T(8,128)(2,1)}, u32[]{:S(2)}) copy-start(bf16[70,8,320]{2,1,0:T(8,128)(2,1)} %param.11) | copy-start | bytes 1075204
  3.5 3.7 %copy-start.3 = (bf16[7168,128]{1,0:T(8,128)(2,1)}, bf16[7168,128]{1,0:T(8,128)(2,1)S(1)}, u32[]{:S(2)}) copy-start(bf16[7168,128]{1,0:T(8,128)(2,1)S(1)} %get-tuple-element.36.xs_own) | copy-start | bytes 5505028
  3.6 13.1 %copy-start.11 = (s32[8,4]{0,1:T(4,128)S(1)}, s32[8,4]{0,1:T(4,128)}, u32[]{:S(2)}) copy-start(s32[8,4]{0,1:T(4,128)} %param.13) | copy-start | bytes 388
  3.6 13.8 %copy-start.8 = (bf16[3,3,96,169]{2,3,1,0:T(8,128)(2,1)S(1)}, bf16[3,3,96,169]{2,3,1,0:T(8,128)(2,1)}, u32[]{:S(2)}) copy-start(bf16[3,3,96,169]{2,3,1,0:T(8,128)(2,1)} %param.16) | copy-start | bytes 876100
  3.6 14.8 %copy-start.9 = (bf16[2,512,64]{1,2,0:T(8,128)(2,1)S(1)}, bf16[2,512,64]{1,2,0:T(8,128)(2,1)}, u32[]{:S(2)}) copy-start(bf16[2,512,64]{1,2,0:T(8,128)(2,1)} %param.15) | copy-start | bytes 393220
  3.6 15.6 %copy-start.10 = (bf16[96,169]{0,1:T(8,128)(2,1)S(1)}, bf16[96,169]{0,1:T(8,128)(2,1)}, u32[]{:S(2)}) copy-start(bf16[96,169]{0,1:T(8,128)(2,1)} %param.20) | copy-start | bytes 97348
  3.6 19.8 %collective-permute-start = (bf16[224,128]{1,0:T(8,128)(2,1)S(1)}, bf16[224,128]{1,0:T(8,128)(2,1)S(1)}, u32[]{:S(2)}, u32[]{:S(2)}) collective-permute-start(bf16[224,128]{1,0:T(8,128)(2,1)S(1)} %get-tuple-element.68), channel_id=1, source_target_pairs={{60,0},{61,1},{62,2},{63,3},{0,4},{1,5},{2,6},{3,7},{4,8},{5,9},{6... | collective-permute-start | bytes 172040 | tf_op jit(solution)/shard_map/ppermute | solution.py:521
  7.3 16.1 %collective-permute-start.1 = (bf16[224,128]{1,0:T(8,128)(2,1)S(1)}, bf16[224,128]{1,0:T(8,128)(2,1)S(1)}, u32[]{:S(2)}, u32[]{:S(2)}) collective-permute-start(bf16[224,128]{1,0:T(8,128)(2,1)S(1)} %get-tuple-element.67), channel_id=1, source_target_pairs={{4,0},{5,1},{6,2},{7,3},{8,4},{9,5},{10,6},{11,7},{12,8},{13,9},{1... | collective-permute-start | bytes 172040 | tf_op jit(solution)/shard_map/ppermute | solution.py:521
  13.1 11.1 %all-to-all-start = ((bf16[8,70,320]{2,1,0:T(8,128)(2,1)}), bf16[8,70,320]{2,1,0:T(8,128)(2,1)S(1)}, u32[]{:S(2)}, u32[]{:S(2)}) async-start(bf16[8,70,320]{2,1,0:T(8,128)(2,1)} %bitcast.32), calls=%async_computation | async-start | bytes 884736 | tf_op jit(solution)/shard_map/all_to_all | solution.py:514
  22.0 15.6 %copy-start.4 = (s32[11]{0:T(128)}, s32[11]{0:T(128)S(1)}, u32[]{:S(2)}) copy-start(s32[11]{0:T(128)S(1)} %stack.51.scal) | copy-start | bytes 136
  23.4 18.0 %copy-start.1 = (bf16[224,128]{1,0:T(8,128)(2,1)}, bf16[224,128]{1,0:T(8,128)(2,1)S(1)}, u32[]{:S(2)}) copy-start(bf16[224,128]{1,0:T(8,128)(2,1)S(1)} %collective-permute-done.above) | copy-start | bytes 172036
  23.4 18.0 %copy-start.2 = (bf16[224,128]{1,0:T(8,128)(2,1)}, bf16[224,128]{1,0:T(8,128)(2,1)S(1)}, u32[]{:S(2)}) copy-start(bf16[224,128]{1,0:T(8,128)(2,1)S(1)} %collective-permute-done.1.below) | copy-start | bytes 172036
  24.1 17.3 %copy-start = (bf16[448,128]{1,0:T(8,128)(2,1)}, bf16[448,128]{1,0:T(8,128)(2,1)S(1)}, u32[]{:S(2)}) copy-start(bf16[448,128]{1,0:T(8,128)(2,1)S(1)} %shard_map.111.ext) | copy-start | bytes 344068
  25.7 19.2 %all-to-all-start.1 = ((bf16[8,72,128]{2,1,0:T(8,128)(2,1)}), bf16[8,72,128]{2,1,0:T(8,128)(2,1)S(1)}, u32[]{:S(2)}, u32[]{:S(2)}) async-start(bf16[8,72,128]{2,1,0:T(8,128)(2,1)} %shard_map.110), calls=%async_computation.1 | async-start | bytes 294912 | tf_op jit(solution)/shard_map/all_to_all | solution.py:514
  35.4 6.0 %collective-permute-start.2 = (bf16[224,128]{1,0:T(8,128)(2,1)S(1)}, bf16[224,128]{1,0:T(8,128)(2,1)S(1)}, u32[]{:S(2)}, u32[]{:S(2)}) collective-permute-start(bf16[224,128]{1,0:T(8,128)(2,1)S(1)} %get-tuple-element.70), channel_id=1, source_target_pairs={{63,0},{0,1},{1,2},{2,3},{3,4},{4,5},{5,6},{6,7},{7,8},{8,9},{9,10... | collective-permute-start | bytes 172040 | tf_op jit(solution)/shard_map/ppermute | solution.py:521
  37.6 3.9 %collective-permute-start.3 = (bf16[224,128]{1,0:T(8,128)(2,1)S(1)}, bf16[224,128]{1,0:T(8,128)(2,1)S(1)}, u32[]{:S(2)}, u32[]{:S(2)}) collective-permute-start(bf16[224,128]{1,0:T(8,128)(2,1)S(1)} %get-tuple-element.69), channel_id=1, source_target_pairs={{1,0},{2,1},{3,2},{4,3},{5,4},{6,5},{7,6},{8,7},{9,8},{10,9},{11,1... | collective-permute-start | bytes 172040 | tf_op jit(solution)/shard_map/ppermute | solution.py:521
  41.5 23.4 %copy-start.12 = (bf16[224,128]{1,0:T(8,128)(2,1)}, bf16[224,128]{1,0:T(8,128)(2,1)S(1)}, u32[]{:S(2)}) copy-start(bf16[224,128]{1,0:T(8,128)(2,1)S(1)} %collective-permute-done.2.west) | copy-start | bytes 172036
  41.5 23.3 %copy-start.13 = (bf16[224,128]{1,0:T(8,128)(2,1)}, bf16[224,128]{1,0:T(8,128)(2,1)S(1)}, u32[]{:S(2)}) copy-start(bf16[224,128]{1,0:T(8,128)(2,1)S(1)} %collective-permute-done.3.east) | copy-start | bytes 172036
  64.4 9.4 %copy-start.6 = (bf16[16,2,72,128]{3,2,1,0:T(8,128)(2,1)}, bf16[16,2,72,128]{3,2,1,0:T(8,128)(2,1)S(1)}, u32[]{:S(2)}) copy-start(bf16[16,2,72,128]{3,2,1,0:T(8,128)(2,1)S(1)} %all_to_all.15) | copy-start | bytes 1769476
  64.4 9.4 %collective-permute-start.4 = (bf16[2304,128]{1,0:T(8,128)(2,1)S(1)}, bf16[2304,128]{1,0:T(8,128)(2,1)}, u32[]{:S(2)}, u32[]{:S(2)}) collective-permute-start(bf16[2304,128]{1,0:T(8,128)(2,1)S(1)} %bitcast.35), channel_id=1, source_target_pairs={{0,1},{1,0},{2,3},{3,2},{4,5},{5,4},{6,7},{7,6},{8,9},{9,8},{10,11... | collective-permute-start | bytes 1769480 | tf_op jit(solution)/shard_map/ppermute | solution.py:581
